TPU v7x, 32 devices: a whole 2x2x4 slice. The times are simulated.
32 devices in a mesh: root: 4 (over z), virt: 4 (over y, x), occ: 2 (over core).
Axes of the slice: x: 2, y: 2, z: 4, core: 2. Of those that a mesh axis runs over, the one named last changes fastest.
Arguments:
- trial_singles: bfloat16 [8, 96], P('root'), may hold values from -6 to 6
- trial_doubles: bfloat16 [8, 480, 9216], P('root', 'virt', 'occ'), may hold values from -6 to 6
- occ_fock: bfloat16 [96, 96], replicated, may hold values from -0.625 to 0.625
- virt_fock: bfloat16 [480, 480], replicated, may hold values from -0.25 to 0.25
- w_ovoo: bfloat16 [96, 480, 9216], P('occ', 'virt', 'root'), may hold values from -0.625 to 0.625
- w_ooov: bfloat16 [96, 480, 9216], P('occ', 'virt', 'root'), may hold values from -0.0029296875 to 0.0029296875
- converged: int32 [8], replicated, may hold values from 0 to 1, as said below
Outputs:
- sigma_doubles: bfloat16 [8, 480, 9216], P('root', 'virt', 'occ')
- sigma_singles: float32 [8, 96], P('root')
- subspace: float32 [8, 8], P('root')
Inputs may be any that keep to these rules, and one draw needn't show every extreme that they name: `converged`: exactly 4 roots are active (0). In every draw at least one aligned block of 2 roots has all its roots active; other blocks may have none.
All inputs are finite; a program needn't handle non-finite values.
Results may differ from a plain program's by a relative error of at most 0.0044.
Values may be sent and summed in bfloat16 or wider, within the bound.
A program may use at most 256 MiB of HBM per device.

v0:
```python
import math

import jax
import jax.numpy as jnp
from jax import lax
from jax.experimental import pallas as pl
from jax.experimental.pallas import tpu as pltpu
from jax.sharding import PartitionSpec as P


def flat_pairs(left, right):
    return lax.dot_general(
        left.reshape(left.shape[0], -1),
        right.reshape(right.shape[0], -1),
        (((1,), (1,)), ((), ())),
        preferred_element_type=jnp.float32,
    )


def plain(trial_singles, trial_doubles, occ_fock, virt_fock, w_ovoo, w_ooov, converged):
    local_roots, virt_local, pair_local = trial_doubles.shape
    occ_count = occ_fock.shape[0]
    virt_count = virt_fock.shape[0]
    root_count = converged.shape[0]
    root_groups = lax.axis_size("root")
    occ_groups = lax.axis_size("occ")
    root_index = lax.axis_index("root")
    occ_index = lax.axis_index("occ")
    occ_half = occ_count // occ_groups
    block_pairs = occ_count * occ_count // root_groups
    own_start = occ_index * occ_half
    active = (1 - converged).astype(jnp.float32)
    own_active = lax.dynamic_slice_in_dim(active, root_index * local_roots, local_roots)
    singles_all = lax.all_gather(trial_singles, "root", axis=0, tiled=True)
    gathered = lax.all_gather(trial_doubles, "occ", axis=2, tiled=True)
    fock_cols = lax.dynamic_slice_in_dim(occ_fock, own_start, occ_half, 1)
    batch_rows = local_roots * virt_local
    stacked = gathered.reshape(batch_rows, occ_count, occ_count)
    first_term = jnp.einsum(
        "ki,bkj->bij", fock_cols, stacked, preferred_element_type=jnp.float32
    ).reshape(local_roots, virt_local, pair_local)
    own_rows = trial_doubles.reshape(batch_rows, occ_half, occ_count)
    second_term = jnp.einsum(
        "bik,kj->bij", own_rows, occ_fock, preferred_element_type=jnp.float32
    ).reshape(local_roots, virt_local, pair_local)
    doubles_block = lax.all_to_all(gathered, "root", split_axis=2, concat_axis=0, tiled=True)
    partial_coupling = flat_pairs(doubles_block, w_ooov)
    coupling_part = lax.dynamic_update_slice(
        jnp.zeros((root_count, occ_count), jnp.float32), partial_coupling, (jnp.int32(0), own_start)
    )
    coupling = lax.psum(coupling_part, ("root", "virt", "occ"))
    singles_fock = jnp.dot(singles_all, occ_fock, preferred_element_type=jnp.float32)
    singles_every = active[:, None] * (-singles_fock - 0.5 * coupling)
    sigma_singles = lax.dynamic_slice_in_dim(singles_every, root_index * local_roots, local_roots)
    singles_cols = lax.dynamic_slice_in_dim(singles_all, own_start, occ_half, 1)
    outer_part = (
        -jnp.dot(singles_cols, w_ovoo.reshape(occ_half, -1), preferred_element_type=jnp.float32)
    ).reshape(root_count, virt_local, block_pairs)
    product = jnp.einsum(
        "ac,ncp->nap",
        virt_fock,
        lax.all_to_all(trial_doubles, "virt", split_axis=2, concat_axis=1, tiled=True),
        preferred_element_type=jnp.float32,
    ).astype(jnp.bfloat16)
    vv_term = lax.all_to_all(product, "virt", split_axis=1, concat_axis=2, tiled=True)
    vv_value = vv_term.astype(jnp.float32)
    outer_own = lax.all_to_all(outer_part, "root", split_axis=0, concat_axis=2, tiled=True)
    outer_half = lax.psum_scatter(outer_own, "occ", scatter_dimension=2, tiled=True)
    summed = vv_value + outer_half - first_term - second_term
    sigma_doubles = (own_active[:, None, None] * summed).astype(jnp.bfloat16)
    trial_piece, sigma_piece = (
        lax.all_to_all(trial_doubles, "root", split_axis=2, concat_axis=0, tiled=True),
        lax.all_to_all(sigma_doubles, "root", split_axis=2, concat_axis=0, tiled=True),
    )
    doubles_part = lax.psum(flat_pairs(trial_piece, sigma_piece), ("root", "virt", "occ"))
    singles_part = jnp.dot(
        singles_all.astype(jnp.float32), singles_every.T, precision=lax.Precision.HIGHEST
    )
    whole_matrix = doubles_part / math.sqrt(
        occ_count * occ_count * virt_count
    ) + singles_part / math.sqrt(occ_count)
    subspace = lax.dynamic_slice_in_dim(whole_matrix, root_index * local_roots, local_roots, 0)
    return (sigma_doubles, sigma_singles, subspace)


ROWS = 8


def call(body, grid, ins, outs, shapes, scratch=(), flops=0, moved=0, semantics=None):
    return pl.pallas_call(
        body,
        grid=grid,
        in_specs=ins,
        out_specs=outs,
        out_shape=shapes,
        scratch_shapes=list(scratch),
        compiler_params=pltpu.CompilerParams(
            dimension_semantics=("arbitrary",) * len(grid), vmem_limit_bytes=48 * 1024 * 1024
        ),
        cost_estimate=pl.CostEstimate(flops=flops, bytes_accessed=moved, transcendentals=0),
    )


SCALAR = pl.BlockSpec(memory_space=pltpu.SMEM)


def rows_flat(block):
    count, rows, width = block.shape
    return block.astype(jnp.float32).reshape(count * rows, width).astype(jnp.bfloat16)


def outer_body(core, mix, weights, kept, sent):
    roots, rows, width = kept.shape
    value = jnp.dot(mix[...], rows_flat(weights[...]), preferred_element_type=jnp.float32)
    value = value.reshape(roots, rows, 2 * width)
    low, high = value[:, :, :width], value[:, :, width:]
    first = core[0] == 0
    kept[...] = jnp.where(first, low, high)
    sent[...] = jnp.where(first, high, low).astype(jnp.bfloat16)


def outer_terms(core, singles_cols, weights):
    count, virt_local, pairs = weights.shape
    roots = singles_cols.shape[0]
    width = pairs // 2
    eye = jnp.eye(ROWS, dtype=jnp.bfloat16)
    mix = (-singles_cols[:, None, :, None] * eye[None, :, None, :]).reshape(
        roots * ROWS, count * ROWS
    )
    piece = pl.BlockSpec((roots, ROWS, width), lambda a: (0, a, 0))
    return call(
        outer_body,
        (virt_local // ROWS,),
        [
            SCALAR,
            pl.BlockSpec(mix.shape, lambda a: (0, 0)),
            pl.BlockSpec((count, ROWS, pairs), lambda a: (0, a, 0)),
        ],
        [piece, piece],
        [
            jax.ShapeDtypeStruct((roots, virt_local, width), jnp.float32),
            jax.ShapeDtypeStruct((roots, virt_local, width), jnp.bfloat16),
        ],
        flops=2 * roots * ROWS * weights.size,
        moved=2 * weights.size,
    )(core, mix, weights)


def coupling_body(core, own, other, weights, total, held):
    width = own.shape[2]

    @pl.when(pl.program_id(0) == 0)
    def _():
        held[...] = jnp.zeros_like(held)

    here = pl.multiple_of(core[0] * width, 128)
    there = pl.multiple_of((1 - core[0]) * width, 128)
    dims = (((1,), (1,)), ((), ()))
    held[...] += lax.dot_general(
        rows_flat(own[...]), rows_flat(weights[:, :, pl.ds(here, width)]), dims,
        preferred_element_type=jnp.float32,
    ) + lax.dot_general(
        rows_flat(other[...]), rows_flat(weights[:, :, pl.ds(there, width)]), dims,
        preferred_element_type=jnp.float32,
    )

    @pl.when(pl.program_id(0) == pl.num_programs(0) - 1)
    def _():
        total[...] = held[...]


def same_row(table, left, rows, right):
    eye = jnp.eye(rows, dtype=jnp.float32)
    return jnp.sum(table.reshape(left, rows, right, rows) * eye[None, :, None, :], axis=(1, 3))


def coupling_sums(core, own, other, weights):
    count, virt_local, pairs = weights.shape
    roots, _, width = own.shape
    shape = (roots * ROWS, count * ROWS)
    piece = pl.BlockSpec((roots, ROWS, width), lambda a: (0, a, 0))
    table = call(
        coupling_body,
        (virt_local // ROWS,),
        [SCALAR, piece, piece, pl.BlockSpec((count, ROWS, pairs), lambda a: (0, a, 0))],
        pl.BlockSpec(shape, lambda a: (0, 0)),
        jax.ShapeDtypeStruct(shape, jnp.float32),
        [pltpu.VMEM(shape, jnp.float32)],
        flops=2 * roots * ROWS * weights.size,
        moved=2 * weights.size,
    )(core, own, other, weights)
    return same_row(table, roots, ROWS, count)


def project_body(left, right, total, held):
    @pl.when(pl.program_id(0) == 0)
    def _():
        held[...] = jnp.zeros_like(held)

    held[...] += lax.dot_general(
        rows_flat(left[...]), rows_flat(right[...]), (((1,), (1,)), ((), ())),
        preferred_element_type=jnp.float32,
    )

    @pl.when(pl.program_id(0) == pl.num_programs(0) - 1)
    def _():
        total[...] = held[...]


def project(left, right):
    roots, virt_local, width = left.shape
    rows = next(n for n in (40, 24, 16, 8) if virt_local % n == 0)
    shape = (roots * rows, roots * rows)
    piece = pl.BlockSpec((roots, rows, width), lambda a: (0, a, 0))
    table = call(
        project_body,
        (virt_local // rows,),
        [piece, piece],
        pl.BlockSpec(shape, lambda a: (0, 0)),
        jax.ShapeDtypeStruct(shape, jnp.float32),
        [pltpu.VMEM(shape, jnp.float32)],
        flops=2 * roots * rows * left.size,
        moved=4 * left.size,
    )(left, right)
    return same_row(table, roots, rows, roots)


def occ_body(tile, count, first, own, other, own_fock, other_fock, unit, second, out):
    column = pl.program_id(0) + first

    def spread(rows):
        parts = [unit[...] * rows[k : k + 1, :] for k in range(rows.shape[0])]
        return jnp.concatenate(parts, axis=0).astype(jnp.bfloat16)

    def step(k, total):
        cut = pl.ds(pl.multiple_of(k * tile, 128), tile)
        total = total + jnp.dot(
            own[:, cut], spread(own_fock[k]), preferred_element_type=jnp.float32
        )
        return total + jnp.dot(
            other[:, cut], spread(other_fock[k]), preferred_element_type=jnp.float32
        )

    here = pl.ds(pl.multiple_of(column * tile, 128), tile)
    begin = jnp.dot(own[:, here], second[...], preferred_element_type=jnp.float32)
    out[...] = lax.fori_loop(0, count, step, begin)


def occ_terms(own, other, fock_own, fock_other, occ_fock, part, parts):
    rows, pairs = own.shape
    occ_count = occ_fock.shape[0]
    group = 128 // math.gcd(occ_count, 128)
    tile = group * occ_count
    count = pairs // tile
    steps = count // parts
    first = part * steps
    eye = jnp.eye(occ_count, dtype=jnp.float32)
    unit = jnp.tile(eye, (1, group))
    second = (
        jnp.eye(group, dtype=jnp.bfloat16)[:, None, :, None] * occ_fock[None, :, None, :]
    ).reshape(tile, tile)

    def wide(block):
        return jnp.repeat(block.astype(jnp.float32), occ_count, axis=1).reshape(count, group, pairs)

    whole = pl.BlockSpec((rows, pairs), lambda c: (0, 0))
    fock_spec = pl.BlockSpec((count, group, tile), lambda c: (0, 0, c + first))

    def body(*refs):
        occ_body(tile, count, first, *refs)

    return call(
        body,
        (steps,),
        [
            whole,
            whole,
            fock_spec,
            fock_spec,
            pl.BlockSpec(unit.shape, lambda c: (0, 0)),
            pl.BlockSpec(second.shape, lambda c: (0, 0)),
        ],
        pl.BlockSpec((rows, tile), lambda c: (0, c)),
        jax.ShapeDtypeStruct((rows, steps * tile), jnp.float32),
        flops=8 * rows * pairs * pairs // parts,
        moved=8 * rows * pairs,
    )(own, other, wide(fock_own), wide(fock_other), unit, second)


def virt_body(fock, amps, out):
    blocks = amps.shape[0]
    for b in range(blocks):
        total = jnp.dot(fock[b, 0], amps[0, 0], preferred_element_type=jnp.float32)
        for c in range(1, blocks):
            total += jnp.dot(fock[b, c], amps[c, 0], preferred_element_type=jnp.float32)
        out[b, 0] = total.astype(jnp.bfloat16)


def virt_product(virt_fock, amps):
    blocks, roots, virt_local, width = amps.shape
    fock = virt_fock.reshape(blocks, virt_local, blocks, virt_local).transpose(0, 2, 1, 3)
    piece = pl.BlockSpec((blocks, 1, virt_local, width), lambda n: (0, n, 0, 0))
    return call(
        virt_body,
        (roots,),
        [pl.BlockSpec(fock.shape, lambda n: (0, 0, 0, 0)), piece],
        piece,
        jax.ShapeDtypeStruct(amps.shape, jnp.bfloat16),
        flops=2 * blocks * virt_local * amps.size,
        moved=4 * amps.size,
    )(fock, amps)


def sigma_body(core, active, vv, mine, theirs, occ_sum, sigma, kept, sent):
    width = mine.shape[3]
    first = core[0] == 0
    weight = active[pl.program_id(0)]
    here = mine[0, 0].astype(jnp.float32)
    there = theirs[0, 0].astype(jnp.float32)
    low = vv[0, 0].astype(jnp.float32) + jnp.where(first, here, there) - occ_sum[0, :, :width]
    high = vv[1, 0].astype(jnp.float32) + jnp.where(first, there, here) - occ_sum[0, :, width:]
    low = weight * low
    high = weight * high
    sigma[0, :, :width] = low.astype(jnp.bfloat16)
    sigma[0, :, width:] = high.astype(jnp.bfloat16)
    kept[0, 0] = jnp.where(first, low, high).astype(jnp.bfloat16)
    sent[0, 0] = jnp.where(first, high, low).astype(jnp.bfloat16)


def sigma_terms(core, active, vv, mine, theirs, occ_sum):
    quarters, roots, virt_local, width = mine.shape
    piece = pl.BlockSpec((1, 1, virt_local, width), lambda n, q: (q, n, 0, 0))
    full = pl.BlockSpec((1, virt_local, 2 * width), lambda n, q: (n, 0, q))
    return call(
        sigma_body,
        (roots, quarters),
        [
            SCALAR,
            SCALAR,
            pl.BlockSpec((2, 1, virt_local, width), lambda n, q: (q, n, 0, 0)),
            piece,
            piece,
            full,
        ],
        [full, piece, piece],
        [
            jax.ShapeDtypeStruct(occ_sum.shape, jnp.bfloat16),
            jax.ShapeDtypeStruct(mine.shape, jnp.bfloat16),
            jax.ShapeDtypeStruct(mine.shape, jnp.bfloat16),
        ],
        flops=8 * occ_sum.size,
        moved=14 * occ_sum.size,
    )(core, active, vv, mine, theirs, occ_sum)


def tiled(trial_doubles, virt_fock, occ_fock):
    _, virt_local, pair_local = trial_doubles.shape
    occ_count = occ_fock.shape[0]
    root_groups = lax.axis_size("root")
    sub = occ_count * occ_count // root_groups // 2
    tile = occ_count * 128 // math.gcd(occ_count, 128)
    return (
        lax.axis_size("occ") == 2
        and root_groups % 2 == 0
        and virt_local % ROWS == 0
        and sub % 128 == 0
        and sub * lax.axis_size("virt") == pair_local
        and pair_local % (2 * tile) == 0
    )


def local(trial_singles, trial_doubles, occ_fock, virt_fock, w_ovoo, w_ooov, converged):
    if not tiled(trial_doubles, virt_fock, occ_fock):
        return plain(trial_singles, trial_doubles, occ_fock, virt_fock, w_ovoo, w_ooov, converged)
    local_roots, virt_local, pair_local = trial_doubles.shape
    occ_count = occ_fock.shape[0]
    virt_count = virt_fock.shape[0]
    root_count = converged.shape[0]
    root_groups = lax.axis_size("root")
    virt_groups = lax.axis_size("virt")
    root_index = lax.axis_index("root")
    occ_index = lax.axis_index("occ")
    occ_half = occ_count // 2
    quarters = root_groups // 2
    sub = pair_local // quarters // 2
    own_start = occ_index * occ_half
    other_start = (1 - occ_index) * occ_half
    core = occ_index.astype(jnp.int32).reshape(1)
    first_core = occ_index == 0
    active = (1 - converged).astype(jnp.float32)
    own_active = lax.dynamic_slice_in_dim(active, root_index * local_roots, local_roots)

    def swap(value):
        return lax.ppermute(value, "occ", [(0, 1), (1, 0)])

    def exchange(value, axis):
        return lax.all_to_all(value, axis, split_axis=0, concat_axis=0, tiled=True)

    def in_order(kept, got):
        return jnp.concatenate(
            [jnp.where(first_core, kept, got), jnp.where(first_core, got, kept)], axis=0
        )

    def own_subs(value):
        return jnp.stack(
            [
                lax.dynamic_slice_in_dim(value, 2 * q * sub + occ_index * sub, sub, 2)
                for q in range(quarters)
            ]
        )

    singles_all = lax.all_gather(trial_singles, "root", axis=0, tiled=True)
    other_doubles = swap(trial_doubles)
    trial_piece = exchange(in_order(own_subs(trial_doubles), own_subs(other_doubles)), "root")
    trial_piece = trial_piece.reshape(root_count, virt_local, sub)
    slabs = jnp.stack(jnp.split(trial_doubles, virt_groups, axis=2))
    slabs = exchange(slabs, "virt")

    singles_cols = lax.dynamic_slice_in_dim(singles_all, own_start, occ_half, 1)
    outer_kept, outer_sent = outer_terms(core, singles_cols, w_ovoo)
    outer_kept, outer_sent, slabs = lax.optimization_barrier((outer_kept, outer_sent, slabs))
    outer_sum = (outer_kept + swap(outer_sent).astype(jnp.float32)).astype(jnp.bfloat16)
    fock_cols = lax.dynamic_slice_in_dim(occ_fock, own_start, occ_half, 1)
    outer_quarters = exchange(
        outer_sum.reshape(root_groups, local_roots, virt_local, sub), "root"
    )

    own_flat = trial_doubles.reshape(local_roots * virt_local, pair_local)
    other_flat = other_doubles.reshape(local_roots * virt_local, pair_local)

    def occ_part(cols, part):
        return occ_terms(
            own_flat,
            other_flat,
            lax.dynamic_slice_in_dim(cols, own_start, occ_half, 0),
            lax.dynamic_slice_in_dim(cols, other_start, occ_half, 0),
            occ_fock,
            part,
            2,
        )

    occ_low = occ_part(fock_cols, 0)
    product = virt_product(virt_fock, slabs)
    product, occ_low, outer_quarters = lax.optimization_barrier((product, occ_low, outer_quarters))
    vv_term = exchange(product, "virt")
    vv_term, fock_cols = lax.optimization_barrier((vv_term, fock_cols))
    occ_high = occ_part(fock_cols, 1)
    occ_sum = jnp.concatenate([occ_low, occ_high], axis=1)
    occ_sum = occ_sum.reshape(local_roots, virt_local, pair_local)

    partial_coupling = coupling_sums(core, trial_piece, swap(trial_piece), w_ooov)
    coupling_part = lax.dynamic_update_slice(
        jnp.zeros((root_count, occ_count), jnp.float32), partial_coupling, (jnp.int32(0), own_start)
    )

    outer_mine = lax.dynamic_slice_in_dim(outer_quarters, quarters * occ_index, quarters)
    outer_theirs = swap(
        lax.dynamic_slice_in_dim(outer_quarters, quarters * (1 - occ_index), quarters)
    )
    sigma_doubles, sigma_kept, sigma_sent = sigma_terms(
        core, own_active, vv_term, outer_mine, outer_theirs, occ_sum
    )
    sigma_piece = exchange(in_order(sigma_kept, swap(sigma_sent)), "root")
    doubles_piece = project(trial_piece, sigma_piece.reshape(root_count, virt_local, sub))

    partial = jnp.concatenate([coupling_part, doubles_piece], axis=1)
    partial = jnp.sum(lax.all_gather(partial, ("root", "virt", "occ")), axis=0)
    coupling, doubles_part = partial[:, :occ_count], partial[:, occ_count:]
    singles_fock = jnp.dot(singles_all, occ_fock, preferred_element_type=jnp.float32)
    singles_every = active[:, None] * (-singles_fock - 0.5 * coupling)
    sigma_singles = lax.dynamic_slice_in_dim(singles_every, root_index * local_roots, local_roots)
    singles_part = jnp.dot(
        singles_all.astype(jnp.float32), singles_every.T, precision=lax.Precision.HIGHEST
    )
    whole_matrix = doubles_part / math.sqrt(
        occ_count * occ_count * virt_count
    ) + singles_part / math.sqrt(occ_count)
    subspace = lax.dynamic_slice_in_dim(whole_matrix, root_index * local_roots, local_roots, 0)
    return (sigma_doubles, sigma_singles, subspace)


def solution(mesh):
    placed = (
        P("root", None),
        P("root", "virt", "occ"),
        P(),
        P(),
        P("occ", "virt", "root"),
        P("occ", "virt", "root"),
        P(),
    )
    return jax.shard_map(
        local,
        mesh=mesh,
        in_specs=placed,
        out_specs=(P("root", "virt", "occ"), P("root", None), P("root", None)),
        check_vma=False,
    )
```

profile of v0, /device:TPU:0, one launch (start us, length us, event | category | flops | bytes accessed | tf_op | source)
XLA Modules:
  0.0 306.6 jit_solution(1009720144404474384)
XLA Ops:
  0.6 3.1 %dynamic-slice_bitcast_fusion.3 = (bf16[1,2,120,1152]{3,2,1,0:T(8,128)(2,1)}, bf16[1,2,120,1152]{3,2,1,0:T(8,128)(2,1)S(1)}, bf16[1,2,120,1152]{3,2,1,0:T(8,128)...) fusion(bf16[2,120,4608]{2,1,0:T(8,128)(2,1)} %param.8, ...), kind=kLoop, calls=%fused_computation.22 | loop fusion | bytes 6635528 | tf_op jit(solution)/shard_map/stack | solution.py:405
  3.8 1.7 pad_maximum_fusion.1
  5.5 5.3 %all-to-all-start = ((bf16[4,2,120,1152]{3,2,1,0:T(8,128)(2,1)}), bf16[4,2,120,1152]{3,2,1,0:T(8,128)(2,1)S(1)}, u32[]{:S(2)}, u32[]{:S(2)}) async-start(bf16[4,2,120,1152]{3,2,1,0:T(8,128)(2,1)} %pad_maximum_fusion.1), calls=%async_computation | async-start | bytes 4423680 | tf_op jit(solution)/shard_map/all_to_all | solution.py:397
  10.8 11.1 %all-gather.1 = bf16[4,2,96]{2,1,0:T(2,128)(2,1)S(1)} all-gather(bf16[1,2,96]{2,1,0:T(2,128)(2,1)S(1)} %bitcast.51), channel_id=1, replica_groups=mesh['root'=4,'virt'=4,'occ'=2] {'root'}, dimensions={0}, use_global_device_ids=true | all-gather | bytes 1920 | tf_op jit(solution)/shard_map/all_gather | solution.py:412
  22.2 0.8 mul.99.mix
  22.9 17.2 %shard_map.94 = (f32[8,120,1152]{2,1,0:T(8,128)}, bf16[8,120,1152]{2,1,0:T(8,128)(2,1)S(1)}) custom-call(s32[1]{0:T(128)} %bitcast.core, bf16[64,384]{1,0:T(8,128)(2,1)S(1)} %mul.99.mix, bf16[48,120,2304]{2,1,0:T(8,128)(2,1)} %weights.2), custom_call_target="tpu_custom_call" | custom-call | flops 1698693120 | bytes 26542080 | tf_op jit(solution)/shard_map/pallas_call | solution.py:131
  40.1 1.4 copy-done.8
  41.6 0.5 collective-permute-start
  42.1 4.0 %collective-permute-done.1 = bf16[8,120,1152]{2,1,0:T(8,128)(2,1)S(1)} collective-permute-done((bf16[8,120,1152]{2,1,0:T(8,128)(2,1)}, bf16[8,120,1152]{2,1,0:T(8,128)(2,1)S(1)}, u32[]{:S(2)}, u32[]{:S(2)}) %collective-permute-start.1) | collective-permute-done | bytes 2211872 | tf_op jit(solution)/shard_map/ppermute | solution.py:394
  46.1 4.2 %add_convert_fusion = bf16[8,120,1152]{2,1,0:T(8,128)(2,1)} fusion(f32[8,120,1152]{2,1,0:T(8,128)} %get-tuple-element.19, bf16[8,120,1152]{2,1,0:T(8,128)(2,1)S(1)} %collective-permute-done.1), kind=kLoop, calls=%fused_computation.1 | loop fusion | flops 3317760 | bytes 8847360 | tf_op jit(solution)/shard_map/convert_element_type | solution.py:422
  50.3 4.6 %all-to-all-start.1 = ((bf16[4,2,120,1152]{3,2,1,0:T(8,128)(2,1)}), bf16[4,2,120,1152]{3,2,1,0:T(8,128)(2,1)}, u32[]{:S(2)}, u32[]{:S(2)}) async-start(bf16[4,2,120,1152]{3,2,1,0:T(8,128)(2,1)} %bitcast.45), calls=%async_computation.1 | async-start | bytes 4423680 | tf_op jit(solution)/shard_map/all_to_all | solution.py:397
  55.4 1.4 broadcast_in_dim.10
  56.8 3.0 reshape_reshape.12.refs_2_
  59.8 1.4 broadcast_in_dim.11
  61.2 3.0 reshape_reshape.13.refs_3_
  64.9 4.0 %shard_map.95 = bf16[4,2,120,1152]{3,2,1,0:T(8,128)(2,1)} custom-call(bf16[4,4,120,120]{3,2,1,0:T(8,128)(2,1)S(1)} %bitcast.43, bf16[4,2,120,1152]{3,2,1,0:T(8,128)(2,1)S(1)} %all-to-all-done.amps), custom_call_target="tpu_custom_call" | custom-call | flops 1061683200 | bytes 4423680 | tf_op jit(solution)/shard_map/pallas_call | solution.py:303
  68.9 36.9 %shard_map.96 = f32[240,2304]{1,0:T(8,128)S(1)} custom-call(bf16[240,4608]{1,0:T(8,128)(2,1)} %bitcast.46, bf16[240,4608]{1,0:T(8,128)(2,1)} %bitcast.9.refs_1_, f32[12,4,4608]{2,1,0:T(4,128)S(1)} %copy-done.2, f32[12,4,4608]{2,1,0:T(4,128)S(1)} %copy-done.3, f32[96,384]{1,0:T(8,128)S(1)} %tile.9.refs_4_, bf16[384,384]{1,0:T(8,128)(2,1)S(1)} %mul.104.refs_5_), custom_call_target="tpu_custom_call" | custom-call | flops 20384317440 | bytes 8847360 | tf_op jit(solution)/shard_map/pallas_call | solution.py:272
  105.7 1.4 copy-done
  107.1 4.3 %all-to-all-start.2 = ((bf16[4,2,120,1152]{3,2,1,0:T(8,128)(2,1)}), bf16[4,2,120,1152]{3,2,1,0:T(8,128)(2,1)S(1)}, u32[]{:S(2)}, u32[]{:S(2)}) async-start(bf16[4,2,120,1152]{3,2,1,0:T(8,128)(2,1)} %shard_map.95), calls=%async_computation.2 | async-start | bytes 4423680 | tf_op jit(solution)/shard_map/all_to_all | solution.py:397
  111.6 1.4 dynamic-slice_bitcast_fusion.1
  113.4 1.6 pad_maximum_fusion.2
  115.0 2.8 constant_dynamic-slice_fusion.2
  117.8 20.1 %all-to-all-done.2.vv = bf16[4,2,120,1152]{3,2,1,0:T(8,128)(2,1)S(1)} async-done(((bf16[4,2,120,1152]{3,2,1,0:T(8,128)(2,1)}), bf16[4,2,120,1152]{3,2,1,0:T(8,128)(2,1)S(1)}, u32[]{:S(2)}, u32[]{:S(2)}) %all-to-all-start.2) | async-done | bytes 2211872 | tf_op jit(solution)/shard_map/all_to_all | solution.py:397
  137.9 1.3 copy-done.9
  139.2 4.7 %all-to-all-start.3 = ((bf16[4,2,120,1152]{3,2,1,0:T(8,128)(2,1)}), bf16[4,2,120,1152]{3,2,1,0:T(8,128)(2,1)S(1)}, u32[]{:S(2)}, u32[]{:S(2)}) async-start(bf16[4,2,120,1152]{3,2,1,0:T(8,128)(2,1)} %pad_maximum_fusion.2), calls=%async_computation.3 | async-start | bytes 4423680 | tf_op jit(solution)/shard_map/all_to_all | solution.py:397
  144.0 1.4 broadcast_in_dim.12
  145.3 3.0 reshape_reshape.14.refs_2_
  148.3 1.4 broadcast_in_dim.13
  149.7 3.0 reshape_reshape.15.refs_3_
  152.7 1.2 copy-done.4
  153.8 1.2 copy-done.5
  155.0 1.0 copy-done.7
  156.0 37.0 %shard_map.97 = f32[240,2304]{1,0:T(8,128)S(1)} custom-call(bf16[240,4608]{1,0:T(8,128)(2,1)} %bitcast.47, bf16[240,4608]{1,0:T(8,128)(2,1)} %bitcast.9.refs_1_, f32[12,4,4608]{2,1,0:T(4,128)S(1)} %copy-done.4, f32[12,4,4608]{2,1,0:T(4,128)S(1)} %copy-done.5, f32[96,384]{1,0:T(8,128)S(1)} %tile.9.refs_4_, bf16[384,384]{1,0:T(8,128)(2,1)S(1)} %copy-done.7), custom_call_target="tpu_custom_call" | custom-call | flops 20384317440 | bytes 8847360 | tf_op jit(solution)/shard_map/pallas_call | solution.py:272
  193.0 2.6 pad_maximum_fusion
  195.6 5.5 %shard_map.98 = (bf16[2,120,4608]{2,1,0:T(8,128)(2,1)}, bf16[2,2,120,1152]{3,2,1,0:T(8,128)(2,1)S(1)}, bf16[2,2,120,1152]{3,2,1,0:T(8,128)(2,1)S(1)}) custom-call(s32[1]{0:T(128)} %bitcast.core, f32[2]{0:T(128)S(1)} %dynamic_slice.45.active, bf16[4,2,120,1152]{3,2,1,0:T(8,128)(2,1)} %copy-done.9, bf16[2,2,120,1152]{3,2,1,0:T(8,128)(2,1)S(1)} %get-tuple-element.42.mine, ...), custom_call_target="tpu_custom_call" | custom-call | flops 8847360 | bytes 15482880 | tf_op jit(solution)/shard_map/pallas_call | solution.py:334
  201.1 2.7 collective-permute-done.4
  204.1 1.6 pad_maximum_fusion.3
  205.7 5.1 %all-to-all-start.4 = ((bf16[4,2,120,1152]{3,2,1,0:T(8,128)(2,1)}), bf16[4,2,120,1152]{3,2,1,0:T(8,128)(2,1)}, u32[]{:S(2)}, u32[]{:S(2)}) async-start(bf16[4,2,120,1152]{3,2,1,0:T(8,128)(2,1)} %pad_maximum_fusion.3), calls=%async_computation.4 | async-start | bytes 4423680 | tf_op jit(solution)/shard_map/all_to_all | solution.py:397
  210.8 4.3 %collective-permute-done.3.other = bf16[8,120,1152]{2,1,0:T(8,128)(2,1)S(1)} collective-permute-done((bf16[8,120,1152]{2,1,0:T(8,128)(2,1)S(1)}, bf16[8,120,1152]{2,1,0:T(8,128)(2,1)S(1)}, u32[]{:S(2)}, u32[]{:S(2)}) %collective-permute-start.3) | collective-permute-done | bytes 2211872 | tf_op jit(solution)/shard_map/ppermute | solution.py:394
  215.1 18.0 %shard_map.99 = f32[64,384]{1,0:T(8,128)S(1)} custom-call(s32[1]{0:T(128)} %bitcast.core, bf16[8,120,1152]{2,1,0:T(8,128)(2,1)S(1)} %bitcast.41, bf16[8,120,1152]{2,1,0:T(8,128)(2,1)S(1)} %collective-permute-done.3.other, bf16[48,120,2304]{2,1,0:T(8,128)(2,1)} %weights.3), custom_call_target="tpu_custom_call" | custom-call | flops 1698693120 | bytes 26542080 | tf_op jit(solution)/shard_map/pallas_call | solution.py:182
  233.1 2.0 reshape.96
  235.1 1.6 multiply_reduce_fusion
  237.0 24.8 %all-to-all-done.4 = bf16[4,2,120,1152]{3,2,1,0:T(8,128)(2,1)} async-done(((bf16[4,2,120,1152]{3,2,1,0:T(8,128)(2,1)}), bf16[4,2,120,1152]{3,2,1,0:T(8,128)(2,1)}, u32[]{:S(2)}, u32[]{:S(2)}) %all-to-all-start.4) | async-done | bytes 2211872 | tf_op jit(solution)/shard_map/all_to_all | solution.py:397
  261.8 3.6 %shard_map.100 = f32[320,320]{1,0:T(8,128)S(1)} custom-call(bf16[8,120,1152]{2,1,0:T(8,128)(2,1)S(1)} %bitcast.42, bf16[8,120,1152]{2,1,0:T(8,128)(2,1)} %bitcast.17.right), custom_call_target="tpu_custom_call" | custom-call | flops 707788800 | bytes 4423680 | tf_op jit(solution)/shard_map/pallas_call | solution.py:215
  265.4 0.5 reshape.98
  266.2 39.0 %all-gather = f32[256,104]{1,0:T(8,128)S(1)} all-gather(f32[8,104]{1,0:T(8,128)S(1)} %pad_maximum_fusion.6), channel_id=2, replica_groups=mesh['root'=4,'virt'=4,'occ'=2] {'root','virt','occ'}, dimensions={0}, use_global_device_ids=true | all-gather | bytes 109824 | tf_op jit(solution)/shard_map/all_gather | solution.py:467
  305.5 0.6 constant_dynamic-slice_fusion.1
  306.1 0.6 constant_dynamic-slice_fusion
  (64 shorter events, 3.0 us)
Async XLA Ops:
  5.5 5.3 %copy-start.15 = (bf16[2,96]{1,0:T(2,128)(2,1)S(1)}, bf16[2,96]{1,0:T(2,128)(2,1)}, u32[]{:S(2)}) copy-start(bf16[2,96]{1,0:T(2,128)(2,1)} %param.7) | copy-start | bytes 1156
  5.5 36.1 %all-to-all-start = ((bf16[4,2,120,1152]{3,2,1,0:T(8,128)(2,1)}), bf16[4,2,120,1152]{3,2,1,0:T(8,128)(2,1)S(1)}, u32[]{:S(2)}, u32[]{:S(2)}) async-start(bf16[4,2,120,1152]{3,2,1,0:T(8,128)(2,1)} %pad_maximum_fusion.1), calls=%async_computation | async-start | bytes 4423680 | tf_op jit(solution)/shard_map/all_to_all | solution.py:397
  40.1 1.4 copy-start.8
  41.5 4.5 %collective-permute-start.1 = (bf16[8,120,1152]{2,1,0:T(8,128)(2,1)}, bf16[8,120,1152]{2,1,0:T(8,128)(2,1)S(1)}, u32[]{:S(2)}, u32[]{:S(2)}) collective-permute-start(bf16[8,120,1152]{2,1,0:T(8,128)(2,1)} %copy-done.8), channel_id=1, source_target_pairs={{0,1},{1,0},{2,3},{3,2},{4,5},{5,4},{6,7},{7,6},{8,9},{9,8},{10,11... | collective-permute-start | bytes 6635528 | tf_op jit(solution)/shard_map/ppermute | solution.py:394
  41.6 27.3 %collective-permute-start = (bf16[2,120,4608]{2,1,0:T(8,128)(2,1)}, bf16[2,120,4608]{2,1,0:T(8,128)(2,1)}, u32[]{:S(2)}, u32[]{:S(2)}) collective-permute-start(bf16[2,120,4608]{2,1,0:T(8,128)(2,1)} %param.8), channel_id=1, source_target_pairs={{0,1},{1,0},{2,3},{3,2},{4,5},{5,4},{6,7},{7,6},{8,9},{9,8},{10,11... | collective-permute-start | bytes 6635528 | tf_op jit(solution)/shard_map/ppermute | solution.py:394
  50.3 4.6 %copy-start.12 = (bf16[480,480]{1,0:T(8,128)(2,1)S(1)}, bf16[480,480]{1,0:T(8,128)(2,1)}, u32[]{:S(2)}) copy-start(bf16[480,480]{1,0:T(8,128)(2,1)} %param.10) | copy-start | bytes 1382404
  50.3 5.1 %copy-start.13 = (bf16[96,96]{1,0:T(8,128)(2,1)S(1)}, bf16[96,96]{1,0:T(8,128)(2,1)}, u32[]{:S(2)}) copy-start(bf16[96,96]{1,0:T(8,128)(2,1)} %param.9) | copy-start | bytes 55300
  50.3 56.9 %all-to-all-start.1 = ((bf16[4,2,120,1152]{3,2,1,0:T(8,128)(2,1)}), bf16[4,2,120,1152]{3,2,1,0:T(8,128)(2,1)}, u32[]{:S(2)}, u32[]{:S(2)}) async-start(bf16[4,2,120,1152]{3,2,1,0:T(8,128)(2,1)} %bitcast.45), calls=%async_computation.1 | async-start | bytes 4423680 | tf_op jit(solution)/shard_map/all_to_all | solution.py:397
  64.6 4.2 %copy-start.6 = (bf16[384,384]{1,0:T(8,128)(2,1)}, bf16[384,384]{1,0:T(8,128)(2,1)S(1)}, u32[]{:S(2)}) copy-start(bf16[384,384]{1,0:T(8,128)(2,1)S(1)} %mul.104.refs_5_) | copy-start | bytes 884740
  64.9 4.0 %copy-start.2 = (f32[12,4,4608]{2,1,0:T(4,128)S(1)}, f32[12,4,4608]{2,1,0:T(4,128)}, u32[]{:S(2)}) copy-start(f32[12,4,4608]{2,1,0:T(4,128)} %reshape_reshape.12.refs_2_) | copy-start | bytes 2654212
  64.9 4.0 %copy-start.3 = (f32[12,4,4608]{2,1,0:T(4,128)S(1)}, f32[12,4,4608]{2,1,0:T(4,128)}, u32[]{:S(2)}) copy-start(f32[12,4,4608]{2,1,0:T(4,128)} %reshape_reshape.13.refs_3_) | copy-start | bytes 2654212
  105.7 1.4 copy-start
  107.1 4.3 %copy-start.16 = (s32[8]{0:T(128)S(1)}, s32[8]{0:T(128)}, u32[]{:S(2)}) copy-start(s32[8]{0:T(128)} %param.13) | copy-start | bytes 100
  107.1 4.4 %copy-start.14 = (bf16[96,96]{1,0:T(8,128)(2,1)S(1)}, bf16[96,96]{1,0:T(8,128)(2,1)}, u32[]{:S(2)}) copy-start(bf16[96,96]{1,0:T(8,128)(2,1)} %param.9) | copy-start | bytes 55300
  107.1 30.7 %all-to-all-start.2 = ((bf16[4,2,120,1152]{3,2,1,0:T(8,128)(2,1)}), bf16[4,2,120,1152]{3,2,1,0:T(8,128)(2,1)S(1)}, u32[]{:S(2)}, u32[]{:S(2)}) async-start(bf16[4,2,120,1152]{3,2,1,0:T(8,128)(2,1)} %shard_map.95), calls=%async_computation.2 | async-start | bytes 4423680 | tf_op jit(solution)/shard_map/all_to_all | solution.py:397
  111.5 1.6 copy-start.10
  111.5 1.6 copy-start.11
  117.8 77.9 %collective-permute-start.2 = (bf16[2,2,120,1152]{3,2,1,0:T(8,128)(2,1)}, bf16[2,2,120,1152]{3,2,1,0:T(8,128)(2,1)}, u32[]{:S(2)}, u32[]{:S(2)}) collective-permute-start(bf16[2,2,120,1152]{3,2,1,0:T(8,128)(2,1)} %get-tuple-element.41), channel_id=1, source_target_pairs={{0,1},{1,0},{2,3},{3,2},{4,5},{5,4},{6,7},{7,6},{8,9},{9,8},{10,11... | collective-permute-start | bytes 3317768 | tf_op jit(solution)/shard_map/ppermute | solution.py:394
  137.9 1.4 copy-start.9
  139.2 66.5 %all-to-all-start.3 = ((bf16[4,2,120,1152]{3,2,1,0:T(8,128)(2,1)}), bf16[4,2,120,1152]{3,2,1,0:T(8,128)(2,1)S(1)}, u32[]{:S(2)}, u32[]{:S(2)}) async-start(bf16[4,2,120,1152]{3,2,1,0:T(8,128)(2,1)} %pad_maximum_fusion.2), calls=%async_computation.3 | async-start | bytes 4423680 | tf_op jit(solution)/shard_map/all_to_all | solution.py:397
  152.7 1.2 copy-start.4
  153.8 1.2 copy-start.5
  155.0 1.0 copy-start.7
  156.0 37.1 %copy-start.1 = (f32[240,2304]{1,0:T(8,128)S(1)}, f32[240,2304]{1,0:T(8,128)}, u32[]{:S(2)}) copy-start(f32[240,2304]{1,0:T(8,128)} %copy-done) | copy-start | bytes 6635524
  201.1 2.7 collective-permute-start.4
  205.7 56.1 %all-to-all-start.4 = ((bf16[4,2,120,1152]{3,2,1,0:T(8,128)(2,1)}), bf16[4,2,120,1152]{3,2,1,0:T(8,128)(2,1)}, u32[]{:S(2)}, u32[]{:S(2)}) async-start(bf16[4,2,120,1152]{3,2,1,0:T(8,128)(2,1)} %pad_maximum_fusion.3), calls=%async_computation.4 | async-start | bytes 4423680 | tf_op jit(solution)/shard_map/all_to_all | solution.py:397
  210.8 4.3 %collective-permute-start.3 = (bf16[8,120,1152]{2,1,0:T(8,128)(2,1)S(1)}, bf16[8,120,1152]{2,1,0:T(8,128)(2,1)S(1)}, u32[]{:S(2)}, u32[]{:S(2)}) collective-permute-start(bf16[8,120,1152]{2,1,0:T(8,128)(2,1)S(1)} %bitcast.40), channel_id=1, source_target_pairs={{0,1},{1,0},{2,3},{3,2},{4,5},{5,4},{6,7},{7,6},{8,9},{9,8},{10,11... | collective-permute-start | bytes 6635528 | tf_op jit(solution)/shard_map/ppermute | solution.py:394
where the time goes:
time: 308 us; the launch traced here: 307 us
  Pallas kernels  122 us (40%)
  waiting for transfers between devices  56 us (18%)
  blocking collectives  50.1 us (16%)
  local copies, waits for them, and re-layouts  37.9 us (12%)
  starting transfers between devices  24.6 us (8%)
  other arithmetic  14.8 us (5%)
    pallas_call x2, Pallas kernels, occ_terms(): call(body, (steps,), [whole, whole, fock_spec, fock_spec, pl.BlockSpec(un...  73.9 us
    all_to_all x5, waiting for transfers between devices, exchange(): return lax.all_to_all(value, axis, split_axis=0, concat_axis=0, tiled=True)  44.9 us
    all_gather x1, blocking collectives, local(): partial = jnp.sum(lax.all_gather(partial, ('root', 'virt', 'occ')), axis=0)  39 us
    all_to_all x5, starting transfers between devices, exchange(): return lax.all_to_all(value, axis, split_axis=0, concat_axis=0, tiled=True)  24.1 us
    pallas_call x1, Pallas kernels, coupling_sums(): call(coupling_body, (virt_local // ROWS,), [SCALAR, piece, piece, pl.Bloc...  18 us
    pallas_call x1, Pallas kernels, outer_terms(): call(outer_body, (virt_local // ROWS,), [SCALAR, pl.BlockSpec(mix.shape,...  17.2 us
    another operation x4, local copies, waits for them, and re-layouts, wide(): jnp.repeat(block.astype(jnp.float32), occ_count, axis=1)  11.9 us
    all_gather x1, blocking collectives, local(): singles_all = lax.all_gather(trial_singles, 'root', axis=0, tiled=True)  11.1 us
  transfers between devices with their start and end apart: 10, of which 5 were waited for; matrix products, arithmetic and copies ran while one was open for 13% of the time, Pallas kernels for 39%

commit v1 on v0

v1 whole, which is shorter than its diff:
```python
import functools
import math

import jax
import jax.numpy as jnp
from jax import lax
from jax.experimental import pallas as pl
from jax.experimental.pallas import tpu as pltpu
from jax.sharding import PartitionSpec as P


def flat_pairs(left, right):
    return lax.dot_general(
        left.reshape(left.shape[0], -1),
        right.reshape(right.shape[0], -1),
        (((1,), (1,)), ((), ())),
        preferred_element_type=jnp.float32,
    )


def plain(trial_singles, trial_doubles, occ_fock, virt_fock, w_ovoo, w_ooov, converged):
    local_roots, virt_local, pair_local = trial_doubles.shape
    occ_count = occ_fock.shape[0]
    virt_count = virt_fock.shape[0]
    root_count = converged.shape[0]
    root_groups = lax.axis_size("root")
    occ_groups = lax.axis_size("occ")
    root_index = lax.axis_index("root")
    occ_index = lax.axis_index("occ")
    occ_half = occ_count // occ_groups
    block_pairs = occ_count * occ_count // root_groups
    own_start = occ_index * occ_half
    active = (1 - converged).astype(jnp.float32)
    own_active = lax.dynamic_slice_in_dim(active, root_index * local_roots, local_roots)
    singles_all = lax.all_gather(trial_singles, "root", axis=0, tiled=True)
    gathered = lax.all_gather(trial_doubles, "occ", axis=2, tiled=True)
    fock_cols = lax.dynamic_slice_in_dim(occ_fock, own_start, occ_half, 1)
    batch_rows = local_roots * virt_local
    stacked = gathered.reshape(batch_rows, occ_count, occ_count)
    first_term = jnp.einsum(
        "ki,bkj->bij", fock_cols, stacked, preferred_element_type=jnp.float32
    ).reshape(local_roots, virt_local, pair_local)
    own_rows = trial_doubles.reshape(batch_rows, occ_half, occ_count)
    second_term = jnp.einsum(
        "bik,kj->bij", own_rows, occ_fock, preferred_element_type=jnp.float32
    ).reshape(local_roots, virt_local, pair_local)
    doubles_block = lax.all_to_all(gathered, "root", split_axis=2, concat_axis=0, tiled=True)
    partial_coupling = flat_pairs(doubles_block, w_ooov)
    coupling_part = lax.dynamic_update_slice(
        jnp.zeros((root_count, occ_count), jnp.float32), partial_coupling, (jnp.int32(0), own_start)
    )
    coupling = lax.psum(coupling_part, ("root", "virt", "occ"))
    singles_fock = jnp.dot(singles_all, occ_fock, preferred_element_type=jnp.float32)
    singles_every = active[:, None] * (-singles_fock - 0.5 * coupling)
    sigma_singles = lax.dynamic_slice_in_dim(singles_every, root_index * local_roots, local_roots)
    singles_cols = lax.dynamic_slice_in_dim(singles_all, own_start, occ_half, 1)
    outer_part = (
        -jnp.dot(singles_cols, w_ovoo.reshape(occ_half, -1), preferred_element_type=jnp.float32)
    ).reshape(root_count, virt_local, block_pairs)
    product = jnp.einsum(
        "ac,ncp->nap",
        virt_fock,
        lax.all_to_all(trial_doubles, "virt", split_axis=2, concat_axis=1, tiled=True),
        preferred_element_type=jnp.float32,
    ).astype(jnp.bfloat16)
    vv_term = lax.all_to_all(product, "virt", split_axis=1, concat_axis=2, tiled=True)
    vv_value = vv_term.astype(jnp.float32)
    outer_own = lax.all_to_all(outer_part, "root", split_axis=0, concat_axis=2, tiled=True)
    outer_half = lax.psum_scatter(outer_own, "occ", scatter_dimension=2, tiled=True)
    summed = vv_value + outer_half - first_term - second_term
    sigma_doubles = (own_active[:, None, None] * summed).astype(jnp.bfloat16)
    trial_piece, sigma_piece = (
        lax.all_to_all(trial_doubles, "root", split_axis=2, concat_axis=0, tiled=True),
        lax.all_to_all(sigma_doubles, "root", split_axis=2, concat_axis=0, tiled=True),
    )
    doubles_part = lax.psum(flat_pairs(trial_piece, sigma_piece), ("root", "virt", "occ"))
    singles_part = jnp.dot(
        singles_all.astype(jnp.float32), singles_every.T, precision=lax.Precision.HIGHEST
    )
    whole_matrix = doubles_part / math.sqrt(
        occ_count * occ_count * virt_count
    ) + singles_part / math.sqrt(occ_count)
    subspace = lax.dynamic_slice_in_dim(whole_matrix, root_index * local_roots, local_roots, 0)
    return (sigma_doubles, sigma_singles, subspace)


ROWS = 8
MESH = pl.DeviceIdType.MESH
HIGH = lax.Precision.HIGHEST
CORES = 2


def flat(block):
    count, rows, width = block.shape
    return block.astype(jnp.float32).reshape(count * rows, width).astype(jnp.bfloat16)


def iota(shape, axis):
    return lax.broadcasted_iota(jnp.int32, shape, axis)


def one_hot(mask, dtype=jnp.float32):
    return jnp.where(mask, 1.0, 0.0).astype(dtype)


def dot(left, right, precision=None):
    return jnp.dot(left, right, preferred_element_type=jnp.float32, precision=precision)


def dot_t(left, right, precision=None):
    return lax.dot_general(
        left, right, (((1,), (1,)), ((), ())),
        preferred_element_type=jnp.float32, precision=precision,
    )


class Sizes:
    def __init__(self, trial_doubles, occ_fock, virt_fock, converged):
        self.local, self.rows, self.pairs = trial_doubles.shape
        self.occ = occ_fock.shape[0]
        self.virt = virt_fock.shape[0]
        self.roots = converged.shape[0]
        self.groups = lax.axis_size("root")
        self.parts = lax.axis_size("virt")
        self.half = self.occ // CORES
        self.per = self.groups // CORES
        self.piece = self.pairs // self.per
        self.slab = self.pairs // self.parts
        self.tiles = self.rows // ROWS
        self.batch = next((g for g in (3, 5, 1) if self.tiles % g == 0))
        self.steps = self.tiles // self.batch
        self.tile = ROWS * self.occ


def fits(trial_doubles, occ_fock, virt_fock, converged):
    s = Sizes(trial_doubles, occ_fock, virt_fock, converged)
    return (
        lax.axis_size("occ") == CORES
        and s.local == CORES
        and s.groups % CORES == 0
        and s.roots == ROWS
        and s.roots == s.local * s.groups
        and s.rows % ROWS == 0
        and s.rows * s.parts == s.virt
        and s.pairs % s.tile == 0
        and s.tile % 128 == 0
        and s.piece % 128 == 0
        and s.slab % 128 == 0
        and s.pairs * CORES == s.occ * s.occ
        and s.occ + s.roots <= 128
    )


def whole_body(
    s, active, singles, trial, flat_trial, occ_fock, virt_fock, ovoo, ooov,
    sigma_out, singles_out, matrix_out,
    sall, mix, unit, second, wide, kron, own, other, slab, product, vv,
    everyone, blocks, kept, sent, got, summed, outer, oo, sigma, sigmas,
    table, square, red0, red1, red2,
    s_one, r_one, s_tri, r_tri, s_fwd, s_own, s_swp, r_swp, s_vin, r_vin, s_vout, r_vout,
    s_blk, s_cor, r_cor, s_out, r_out, s_sig, r_sig, s_res, s_red, r_red,
):
    z, v, c = lax.axis_index("root"), lax.axis_index("virt"), lax.axis_index("occ")
    mate = 1 - c
    groups, parts, per, batch = s.groups, s.parts, s.per, s.batch
    home, place = z // per, z % per
    at_home = home == c

    def turn(index, by, size):
        return lax.rem(index + by, size)

    def remote(src, dst, send, recv, **where):
        return pltpu.make_async_remote_copy(
            src_ref=src, dst_ref=dst, send_sem=send, recv_sem=recv,
            device_id=where, device_id_type=MESH,
        )

    def lanes(index, width):
        return pl.ds(pl.multiple_of(index * width, 128), width)

    def cut(t):
        return pl.ds(t * batch, batch)

    def one_copy(d):
        to = turn(z, d, groups)
        return remote(sall.at[z], sall.at[z], s_one.at[d], r_one.at[z], root=to)

    def one_got(d):
        src = turn(z, d, groups)
        return remote(sall.at[src], sall.at[src], s_one.at[d], r_one.at[src], root=src)

    def trial_copy(j, r):
        to = c * per + j
        core = jnp.where(to == z, mate, r)
        n = z * s.local + r
        return remote(
            trial.at[r, :, :, lanes(j, s.piece)], everyone.at[n],
            s_tri.at[j, r], r_tri.at[n], root=to, occ=core,
        )

    def trial_own(r):
        n = z * s.local + r
        return pltpu.make_async_copy(
            trial.at[r, :, :, lanes(place, s.piece)], everyone.at[n], r_tri.at[n]
        )

    def trial_pass(d):
        n = turn(z, d, groups) * s.local + c
        return remote(everyone.at[n], everyone.at[n], s_fwd.at[d], r_tri.at[n], occ=mate)

    def trial_got(n):
        return remote(everyone.at[n], everyone.at[n], s_fwd.at[0], r_tri.at[n], occ=mate)

    def swap_copy():
        return remote(flat_trial, other, s_swp, r_swp, occ=mate)

    def slab_rows(u):
        return pl.ds(u * s.tiles, s.tiles)

    def slab_copy(d, r):
        u = turn(v, d, parts)
        return remote(
            trial.at[r, :, :, lanes(u, s.slab)], slab.at[r, slab_rows(v)],
            s_vin.at[d, r], r_vin.at[v, r], virt=u,
        )

    def slab_own(r):
        return pltpu.make_async_copy(
            trial.at[r, :, :, lanes(v, s.slab)], slab.at[r, slab_rows(v)], r_vin.at[v, r]
        )

    def slab_got(d, r):
        u = turn(v, d, parts)
        return remote(
            slab.at[r, slab_rows(u)], slab.at[r, slab_rows(u)],
            s_vin.at[d, r], r_vin.at[u, r], virt=u,
        )

    def back_copy(d, r):
        u = turn(v, d, parts)
        return remote(
            product.at[d, r], vv.at[r, :, :, lanes(v, s.slab)],
            s_vout.at[d, r], r_vout.at[v, r], virt=u,
        )

    def back_got(d, r):
        u = turn(v, d, parts)
        return remote(
            product.at[d, r], vv.at[r, :, :, lanes(u, s.slab)],
            s_vout.at[d, r], r_vout.at[u, r], virt=u,
        )

    def load(source, t, slot):
        return pltpu.make_async_copy(
            source.at[:, cut(t)], blocks.at[slot], s_blk.at[slot]
        )

    def core_copy(t):
        return remote(
            sent.at[:, cut(t)], got.at[:, cut(t)], s_cor.at[t], r_cor.at[t], occ=mate
        )

    def outer_copy(t, d):
        to = turn(z, d, groups)
        return remote(
            summed.at[to, cut(t)], outer.at[c, cut(t), :, lanes(place, s.piece)],
            s_out.at[t, d], r_out.at[t, place, c], root=to, occ=home,
        )

    def outer_got(t, j, r):
        src = c * per + j
        core = jnp.where(src == z, mate, r)
        spot = outer.at[r, cut(t), :, lanes(j, s.piece)]
        return remote(spot, spot, s_out.at[t, 0], r_out.at[t, j, r], root=src, occ=core)

    def sigma_copy(t, r, j):
        to = c * per + j
        return remote(
            sigma.at[r, cut(t), :, lanes(j, s.piece)], sigmas.at[z, cut(t)],
            s_sig.at[t, r, j], r_sig.at[t, z], root=to, occ=r,
        )

    def sigma_got(t, d):
        src = turn(z, d, groups)
        core = jnp.where(src == z, mate, home)
        return remote(
            sigmas.at[src, cut(t)], sigmas.at[src, cut(t)],
            s_sig.at[t, 0, 0], r_sig.at[t, src], root=src, occ=core,
        )

    def result_copy(t, r):
        return pltpu.make_async_copy(
            sigma.at[r, cut(t)], sigma_out.at[r, cut(t)], s_res.at[t, r]
        )

    barrier = pltpu.get_barrier_semaphore()
    greeted = 0
    for d in range(groups):
        for e in range(CORES):
            if d or e:
                pl.semaphore_signal(
                    barrier, inc=1, device_id_type=MESH,
                    device_id={"root": turn(z, d, groups), "occ": turn(c, e, CORES)},
                )
                greeted += 1
    for d in range(1, parts):
        pl.semaphore_signal(
            barrier, inc=1, device_id_type=MESH, device_id={"virt": turn(v, d, parts)}
        )
        greeted += 1
    load(ovoo, 0, 0).start()
    row = iota((ROWS, 128), 0)
    mine = jnp.zeros((ROWS, 128), jnp.float32)
    wide_ones = jnp.concatenate(
        [singles[...].astype(jnp.float32), jnp.zeros((s.local, 128 - s.occ), jnp.float32)], axis=1
    )
    for r in range(s.local):
        mine = jnp.where(row == z * s.local + r, wide_ones[r : r + 1, :], mine)
    sall[z] = mine
    pl.semaphore_wait(barrier, greeted)

    for d in range(1, groups):
        one_copy(d).start()
    for j in range(per):
        for r in range(s.local):
            trial_copy(j, r).start()

    @pl.when(at_home)
    def _():
        for r in range(s.local):
            trial_own(r).start()

    for r in range(s.local):
        for d in range(1, parts):
            slab_copy(d, r).start()
        slab_own(r).start()
    swap_copy().start()
    own_copy = pltpu.make_async_copy(flat_trial, own, s_own)
    own_copy.start()

    line = iota((s.occ, s.tile), 0)
    lane = iota((s.occ, s.tile), 1)
    spots = line == lane
    for i in range(1, ROWS):
        spots = spots | (line + i * s.occ == lane)
    unit[...] = one_hot(spots)
    spread_fock = dot(occ_fock[...], unit[...].astype(jnp.bfloat16))
    for i in range(ROWS):
        inside = (lane >= i * s.occ) & (lane < (i + 1) * s.occ)
        second[i * s.occ : (i + 1) * s.occ, :] = jnp.where(inside, spread_fock, 0.0).astype(
            jnp.bfloat16
        )

    def widen(col, carry):
        first = (line - c * s.half) * s.occ - col * s.tile
        pick = (lane >= first) & (lane < first + s.occ)
        wide[:, lanes(col, s.tile)] = dot(occ_fock[...], one_hot(pick, jnp.bfloat16))
        return carry

    columns = s.pairs // s.tile
    lax.fori_loop(0, columns, widen, 0)

    for d in range(1, groups):
        one_got(d).wait_recv()
    everyones = sall[0]
    for g in range(1, groups):
        everyones = everyones + sall[g]
    left = iota((s.roots * ROWS, s.roots), 0) // ROWS
    chosen = jnp.where(
        left < groups, s.local * left + c, s.local * (left - groups) + mate
    )
    left = one_hot(iota((s.roots * ROWS, s.roots), 1) == chosen, jnp.bfloat16)
    right = iota((128, s.half * ROWS), 1) // ROWS + c * s.half
    right = one_hot(iota((128, s.half * ROWS), 0) == right, jnp.bfloat16)
    shape = (s.roots * ROWS, s.half * ROWS)
    mixed = dot(dot(left, everyones.astype(jnp.bfloat16)).astype(jnp.bfloat16), right)
    same = iota(shape, 0) % ROWS == iota(shape, 1) % ROWS
    mix[...] = jnp.where(same, -mixed, 0.0).astype(jnp.bfloat16)

    def finish(t):
        core_copy(t).wait_recv()
        slot = lax.rem(t, 2)
        for g in range(batch):
            tile = t * batch + g
            summed[:, tile] = (kept[slot, :, g] + got[:, tile].astype(jnp.float32)).astype(
                jnp.bfloat16
            )
        for d in range(1, groups):
            outer_copy(t, d).start()

        @pl.when(at_home)
        def _():
            for g in range(batch):
                tile = t * batch + g
                outer[c, tile, :, lanes(place, s.piece)] = summed[z, tile]

        @pl.when(jnp.logical_not(at_home))
        def _():
            outer_copy(t, 0).start()

    def outer_step(t, carry):
        slot = lax.rem(t, 2)

        @pl.when(t + 1 < s.steps)
        def _():
            load(ovoo, t + 1, 1 - slot).start()

        load(ovoo, t, slot).wait()
        for g in range(batch):
            value = dot(mix[...], flat(blocks[slot, :, g]))
            value = value.reshape(s.roots, ROWS, s.piece)
            kept[slot, :, g] = value[:groups]
            sent[:, t * batch + g] = value[groups:].astype(jnp.bfloat16)
        core_copy(t).start()

        @pl.when(t > 0)
        def _():
            finish(t - 1)

        return carry

    lax.fori_loop(0, s.steps, outer_step, 0)
    finish(s.steps - 1)
    load(ooov, 0, 0).start()

    own_copy.wait()
    swap_copy().wait_recv()

    def spread(half, k, here):
        start = pl.multiple_of(half * s.half + k * ROWS, ROWS)
        rows = wide[pl.ds(start, ROWS), here]
        for i in range(ROWS):
            kron[i * s.occ : (i + 1) * s.occ, :] = (unit[...] * rows[i : i + 1, :]).astype(
                jnp.bfloat16
            )

    def column(col, carry):
        here = lanes(col, s.tile)
        oo[:, here] = dot(own[:, here], second[...])

        def inner(k, carry):
            there = lanes(k, s.tile)
            spread(c, k, here)
            oo[:, here] += dot(own[:, there], kron[...])
            spread(mate, k, here)
            oo[:, here] += dot(other[:, there], kron[...])
            return carry

        return lax.fori_loop(0, columns, inner, carry)

    early = columns // 3
    lax.fori_loop(0, early, column, 0)
    for r in range(s.local):
        for d in range(1, parts):
            slab_got(d, r).wait_recv()
        slab_own(r).wait()
    for r in range(s.local):
        amps = flat(slab[r])
        for d in range(1, parts):
            part = dot(virt_fock[turn(v, d, parts)], amps)
            product[d, r] = part.reshape(s.tiles, ROWS, s.slab).astype(jnp.bfloat16)
            back_copy(d, r).start()
        part = dot(virt_fock[v], amps).reshape(s.tiles, ROWS, s.slab)
        vv[r, :, :, lanes(v, s.slab)] = part.astype(jnp.bfloat16)
    lax.fori_loop(early, columns, column, 0)

    for d in range(1, groups):
        trial_got(turn(z, d, groups) * s.local + c).wait_recv()
        trial_pass(d).start()
    for r in range(s.local):
        for d in range(1, parts):
            back_got(d, r).wait_recv()

    def sigma_step(t, carry):
        for r in range(s.local):
            for j in range(per):
                @pl.when(jnp.logical_not((c * per + j == z) & (c == r)))
                def _():
                    outer_got(t, j, r).wait_recv()

            for g in range(batch):
                tile = t * batch + g
                rows = pl.ds(pl.multiple_of(r * s.rows + tile * ROWS, ROWS), ROWS)
                value = (
                    vv[r, tile].astype(jnp.float32)
                    + outer[r, tile].astype(jnp.float32)
                    - oo[rows, :]
                )
                sigma[r, tile] = (active[z * s.local + r] * value).astype(jnp.bfloat16)
            result_copy(t, r).start()
            for j in range(per):
                here = (c * per + j == z) & (c == r)

                @pl.when(jnp.logical_not(here))
                def _():
                    sigma_copy(t, r, j).start()

                @pl.when(here)
                def _():
                    for g in range(batch):
                        tile = t * batch + g
                        sigmas[z, tile] = sigma[r, tile, :, j * s.piece : (j + 1) * s.piece]

        return carry

    lax.fori_loop(0, s.steps, sigma_step, 0)

    for d in range(1, groups):
        trial_got(turn(z, d, groups) * s.local + mate).wait_recv()
    for r in range(s.local):
        trial_got(z * s.local + r).wait_recv()
    table[...] = jnp.zeros_like(table)
    square[...] = jnp.zeros_like(square)

    def coupling_step(t, carry):
        slot = lax.rem(t, 2)

        @pl.when(t + 1 < s.steps)
        def _():
            load(ooov, t + 1, 1 - slot).start()

        load(ooov, t, slot).wait()
        for g in range(batch):
            table[...] += dot_t(flat(everyone[:, t * batch + g]), flat(blocks[slot, :, g]))
        return carry

    lax.fori_loop(0, s.steps, coupling_step, 0)

    def project_step(t, carry):
        for d in range(groups):
            if d:
                sigma_got(t, d).wait_recv()
            else:
                @pl.when(jnp.logical_not(at_home))
                def _():
                    sigma_got(t, 0).wait_recv()

        for g in range(batch):
            tile = t * batch + g
            square[...] += dot_t(flat(everyone[:, tile]), flat(sigmas[:, tile]))
        return carry

    lax.fori_loop(0, s.steps, project_step, 0)

    gather = one_hot(iota((s.roots, s.roots * ROWS), 1) // ROWS == iota((s.roots, s.roots * ROWS), 0))

    def same_row(values, target):
        rows = iota(values.shape, 0) % ROWS == iota(values.shape, 1) % ROWS
        folded = dot(gather, jnp.where(rows, values, 0.0), HIGH)
        width = values.shape[1]
        to = target(iota((width, 128), 0) // ROWS)
        return dot(folded, one_hot(iota((width, 128), 1) == to), HIGH)

    part = same_row(table[...], lambda k: c * s.half + k)
    part = part + same_row(square[...], lambda o: s.occ + s.local * o + c)

    def summed_over(held, index, size, base, name):
        def copy(d):
            return remote(
                held.at[index], held.at[index], s_red.at[base + d], r_red.at[base + index],
                **{name: turn(index, d, size)},
            )

        def got_from(d):
            src = turn(index, d, size)
            return remote(
                held.at[src], held.at[src], s_red.at[base + d], r_red.at[base + src],
                **{name: src},
            )

        for d in range(1, size):
            copy(d).start()
        for d in range(1, size):
            got_from(d).wait_recv()
        total = held[0]
        for g in range(1, size):
            total = total + held[g]
        return total, copy

    red0[c] = part
    total, copy0 = summed_over(red0, c, CORES, 0, "occ")
    red1[v] = total
    total, copy1 = summed_over(red1, v, parts, CORES, "virt")
    red2[z] = total
    total, copy2 = summed_over(red2, z, groups, CORES + parts, "root")

    coupling = total[:, : s.occ]
    ones = everyones[:, : s.occ]
    weight = jnp.zeros((s.roots, 1), jnp.float32)
    for n in range(s.roots):
        weight = jnp.where(iota((s.roots, 1), 0) == n, active[n], weight)
    every = weight * (-dot(ones.astype(jnp.bfloat16), occ_fock[...]) - 0.5 * coupling)
    whole = total[:, s.occ : s.occ + s.roots] / math.sqrt(s.occ * s.occ * s.virt)
    whole = whole + dot_t(ones, every, HIGH) / math.sqrt(s.occ)
    pick = one_hot(
        iota((s.local, s.roots), 1) == iota((s.local, s.roots), 0) + z * s.local
    )
    singles_out[...] = dot(pick, every, HIGH)
    matrix_out[...] = dot(pick, whole, HIGH)

    for d in range(1, groups):
        one_copy(d).wait_send()
        trial_pass(d).wait_send()
        copy2(d).wait_send()
    for d in range(1, parts):
        copy1(d).wait_send()
        for r in range(s.local):
            slab_copy(d, r).wait_send()
            back_copy(d, r).wait_send()
    copy0(1).wait_send()
    swap_copy().wait_send()
    for j in range(per):
        for r in range(s.local):
            trial_copy(j, r).wait_send()

    def drain(t, carry):
        core_copy(t).wait_send()
        for d in range(1, groups):
            outer_copy(t, d).wait_send()

        @pl.when(jnp.logical_not(at_home))
        def _():
            outer_copy(t, 0).wait_send()

        for r in range(s.local):
            result_copy(t, r).wait()
            for j in range(per):
                @pl.when(jnp.logical_not((c * per + j == z) & (c == r)))
                def _():
                    sigma_copy(t, r, j).wait_send()

        return carry

    lax.fori_loop(0, s.steps, drain, 0)


def local(trial_singles, trial_doubles, occ_fock, virt_fock, w_ovoo, w_ooov, converged):
    if not fits(trial_doubles, occ_fock, virt_fock, converged):
        return plain(trial_singles, trial_doubles, occ_fock, virt_fock, w_ovoo, w_ooov, converged)
    s = Sizes(trial_doubles, occ_fock, virt_fock, converged)
    active = (1 - converged).astype(jnp.float32)
    trial = trial_doubles.reshape(s.local, s.tiles, ROWS, s.pairs)
    flat_trial = trial_doubles.reshape(s.local * s.rows, s.pairs)
    fock = virt_fock.reshape(s.parts, s.rows, s.virt)
    outer_in = w_ovoo.reshape(s.half, s.tiles, ROWS, s.piece)
    coupling_in = w_ooov.reshape(s.half, s.tiles, ROWS, s.piece)
    bf, f32 = jnp.bfloat16, jnp.float32
    anywhere = pl.BlockSpec(memory_space=pl.ANY)
    vmem = pl.BlockSpec(memory_space=pltpu.VMEM)
    smem = pl.BlockSpec(memory_space=pltpu.SMEM)
    dma, n = pltpu.SemaphoreType.DMA, s.roots * ROWS
    wide_tile = (s.tiles, ROWS, s.piece)
    sigma, singles, matrix = pl.pallas_call(
        functools.partial(whole_body, s),
        in_specs=[smem, vmem, anywhere, anywhere, vmem, vmem, anywhere, anywhere],
        out_specs=[anywhere, vmem, vmem],
        out_shape=[
            jax.ShapeDtypeStruct(trial.shape, bf),
            jax.ShapeDtypeStruct((s.local, s.occ), f32),
            jax.ShapeDtypeStruct((s.local, s.roots), f32),
        ],
        scratch_shapes=[
            pltpu.VMEM((s.groups, ROWS, 128), f32),
            pltpu.VMEM((n, s.half * ROWS), bf),
            pltpu.VMEM((s.occ, s.tile), f32),
            pltpu.VMEM((s.tile, s.tile), bf),
            pltpu.VMEM((s.occ, s.pairs), f32),
            pltpu.VMEM((s.tile, s.tile), bf),
            pltpu.VMEM(flat_trial.shape, bf),
            pltpu.VMEM(flat_trial.shape, bf),
            pltpu.VMEM((s.local, s.parts * s.tiles, ROWS, s.slab), bf),
            pltpu.VMEM((s.parts, s.local, s.tiles, ROWS, s.slab), bf),
            pltpu.VMEM(trial.shape, bf),
            pltpu.VMEM((s.roots,) + wide_tile, bf),
            pltpu.VMEM((2, s.half, s.batch, ROWS, s.piece), bf),
            pltpu.VMEM((2, s.groups, s.batch, ROWS, s.piece), f32),
            pltpu.VMEM((s.groups,) + wide_tile, bf),
            pltpu.VMEM((s.groups,) + wide_tile, bf),
            pltpu.VMEM((s.groups,) + wide_tile, bf),
            pltpu.VMEM(trial.shape, bf),
            pltpu.VMEM(flat_trial.shape, f32),
            pltpu.VMEM(trial.shape, bf),
            pltpu.VMEM((s.groups,) + wide_tile, bf),
            pltpu.VMEM((n, s.half * ROWS), f32),
            pltpu.VMEM((n, s.groups * ROWS), f32),
            pltpu.VMEM((CORES, ROWS, 128), f32),
            pltpu.VMEM((s.parts, ROWS, 128), f32),
            pltpu.VMEM((s.groups, ROWS, 128), f32),
            dma((s.groups,)), dma((s.groups,)),
            dma((s.per, s.local)), dma((s.roots,)), dma((s.groups,)), dma(()),
            dma(()), dma(()),
            dma((s.parts, s.local)), dma((s.parts, s.local)),
            dma((s.parts, s.local)), dma((s.parts, s.local)),
            dma((2,)), dma((s.steps,)), dma((s.steps,)),
            dma((s.steps, s.groups)), dma((s.steps, s.per, s.local)),
            dma((s.steps, s.local, s.per)), dma((s.steps, s.groups)),
            dma((s.steps, s.local)),
            dma((CORES + s.parts + s.groups,)), dma((CORES + s.parts + s.groups,)),
        ],
        compiler_params=pltpu.CompilerParams(
            collective_id=0, has_side_effects=True, vmem_limit_bytes=66 * 1000 * 1000
        ),
        cost_estimate=pl.CostEstimate(
            flops=8 * s.rows * s.pairs * s.pairs, bytes_accessed=4 * w_ovoo.size, transcendentals=0
        ),
        name="sigma_step",
    )(active, trial_singles, trial, flat_trial, occ_fock, fock, outer_in, coupling_in)
    return (sigma.reshape(trial_doubles.shape), singles, matrix)


def solution(mesh):
    placed = (
        P("root", None),
        P("root", "virt", "occ"),
        P(),
        P(),
        P("occ", "virt", "root"),
        P("occ", "virt", "root"),
        P(),
    )
    return jax.shard_map(
        local,
        mesh=mesh,
        in_specs=placed,
        out_specs=(P("root", "virt", "occ"), P("root", None), P("root", None)),
        check_vma=False,
    )
```

time: 308 us -> 169 us (0.55)
  waiting for transfers between devices: 56 us -> 0 us
  blocking collectives: 50.1 us -> 0 us
  Pallas kernels: 122 us -> 163 us
  local copies, waits for them, and re-layouts: 37.9 us -> 4.26 us
  starting transfers between devices: 24.6 us -> 0 us
  other arithmetic: 14.8 us -> 1.17 us
    all_gather x2 -> x0, blocking collectives: 50.1 us -> none  [the longest x1 39 us: local(): partial = jnp.sum(lax.all_gather(partial, ('root', 'virt', 'occ')), axis=0)]
    all_to_all x5 -> x0, waiting for transfers between devices: 44.9 us -> none  [exchange(): return lax.all_to_all(value, axis, split_axis=0, concat_axis=0, tiled=True)]
    pallas_call x7 -> x1, Pallas kernels: 122 us -> 163 us  [local(): pl.pallas_call(functools.partial(whole_body, s), in_specs=[smem, vmem, an...]
    all_to_all x5 -> x0, starting transfers between devices: 24.1 us -> none  [exchange(): return lax.all_to_all(value, axis, split_axis=0, concat_axis=0, tiled=True)]
    another operation x8 -> x0, local copies, waits for them, and re-layouts: 16.6 us -> none  [the longest x4 11.9 us: wide(): jnp.repeat(block.astype(jnp.float32), occ_count, axis=1)]
    ppermute x5 -> x0, waiting for transfers between devices: 11.1 us -> none  [swap(): return lax.ppermute(value, 'occ', [(0, 1), (1, 0)])]
    concatenate x4 -> x0, other arithmetic: 5.92 us -> none  [the longest x2 3.24 us: in_order(): jnp.concatenate([jnp.where(first_core, kept, got), jnp.where(first_core,...]
    broadcast_in_dim x5 -> x0, local copies, waits for them, and re-layouts: 5.53 us -> none  [the longest x4 5.53 us: wide(): jnp.repeat(block.astype(jnp.float32), occ_count, axis=1)]
  transfers between devices with their start and end apart: 10 -> 0, of which waited for: 5 -> 0; matrix products, arithmetic and copies ran while one was open for 13% -> 0% of each run, Pallas kernels for 39% -> 0%
where the time goes in v1:
time: 169 us
  Pallas kernels  163 us (96%)
  local copies, waits for them, and re-layouts  4.26 us (3%)
    pallas_call x1, Pallas kernels, local(): pl.pallas_call(functools.partial(whole_body, s), in_specs=[smem, vmem, an...  163 us
    unnamed x7, local copies, waits for them, and re-layouts  4.26 us

profile of v1, /device:TPU:0, one launch (start us, length us, event | category | flops | bytes accessed | tf_op | source)
XLA Modules:
  0.0 168.9 jit_solution(18379550862236601493)
XLA Ops:
  0.6 1.2 subtract_convert_fusion.active
  1.8 162.8 %sigma_step.1 = (bf16[2,15,8,4608]{3,2,1,0:T(8,128)(2,1)}, f32[2,96]{1,0:T(2,128)}, f32[2,8]{1,0:T(2,128)}) custom-call(f32[8]{0:T(128)} %subtract_convert_fusion.active, bf16[2,96]{1,0:T(2,128)(2,1)} %singles.1, bf16[2,15,8,4608]{3,2,1,0:T(8,128)(2,1)} %bitcast.9, bf16[240,4608]{1,0:T(8,128)(2,1)} %bitcast.10, bf16[96,96]{1,0:T(8,128)(2,1)} %occ_fock.1, ...), custom_call_target="tpu_custom_call" | custom-call | flops 20384317440 | bytes 53084160 | tf_op jit(solution)/shard_map/sigma_step/pallas_call | solution.py:653
  164.6 0.0 copy-start.1
  164.6 0.0 copy-start
  164.6 3.1 %copy.13 = bf16[2,120,4608]{2,1,0:T(8,128)(2,1)} copy(bf16[2,120,4608]{2,1,0:T(8,128)(2,1)} %bitcast.6) | data formatting | bytes 4423680
  167.8 0.0 copy-done.1
  167.8 0.6 copy.14
  168.3 0.0 copy-done
  168.3 0.6 copy.15
Async XLA Ops:
  164.6 3.1 %copy-start.1 = (f32[2,96]{1,0:T(2,128)S(1)}, f32[2,96]{1,0:T(2,128)}, u32[]{:S(2)}) copy-start(f32[2,96]{1,0:T(2,128)} %get-tuple-element.13) | copy-start | bytes 2308
  164.6 3.7 %copy-start = (f32[2,8]{1,0:T(2,128)S(1)}, f32[2,8]{1,0:T(2,128)}, u32[]{:S(2)}) copy-start(f32[2,8]{1,0:T(2,128)} %get-tuple-element.14) | copy-start | bytes 196

commit v2 on v1

--- a/solution.py
+++ b/solution.py
@@ -125,11 +125,13 @@
         self.half = self.occ // CORES
         self.per = self.groups // CORES
         self.piece = self.pairs // self.per
-        self.slab = self.pairs // self.parts
+        self.slots = self.roots // 2
         self.tiles = self.rows // ROWS
         self.batch = next((g for g in (3, 5, 1) if self.tiles % g == 0))
         self.steps = self.tiles // self.batch
         self.tile = ROWS * self.occ
+        self.thirds = self.piece // self.tile
+        self.slab = self.tile // CORES
 
 
 def fits(trial_doubles, occ_fock, virt_fock, converged):
@@ -137,14 +139,13 @@
     return (
         lax.axis_size("occ") == CORES
         and s.local == CORES
-        and s.groups % CORES == 0
+        and s.groups == 4
+        and s.parts == 4
         and s.roots == ROWS
         and s.roots == s.local * s.groups
         and s.rows % ROWS == 0
         and s.rows * s.parts == s.virt
-        and s.pairs % s.tile == 0
-        and s.tile % 128 == 0
-        and s.piece % 128 == 0
+        and s.piece % s.tile == 0
         and s.slab % 128 == 0
         and s.pairs * CORES == s.occ * s.occ
         and s.occ + s.roots <= 128
@@ -152,19 +153,54 @@
 
 
 def whole_body(
-    s, active, singles, trial, flat_trial, occ_fock, virt_fock, ovoo, ooov,
+    s, converged, singles, trial, flat_trial, occ_fock, virt_fock, ovoo, ooov,
     sigma_out, singles_out, matrix_out,
     sall, mix, unit, second, wide, kron, own, other, slab, product, vv,
-    everyone, blocks, kept, sent, got, summed, outer, oo, sigma, sigmas,
+    everyone, blocks, kept, sent, got, summed, oo, sigma,
+    rest, near, across, far, handed, taken,
     table, square, red0, red1, red2,
     s_one, r_one, s_tri, r_tri, s_fwd, s_own, s_swp, r_swp, s_vin, r_vin, s_vout, r_vout,
-    s_blk, s_cor, r_cor, s_out, r_out, s_sig, r_sig, s_res, s_red, r_red,
+    s_blk, s_cor, r_cor, s_near, r_near, s_far, r_far, s_pass, r_pass, s_hand, r_hand,
+    s_res, s_red, r_red,
 ):
     z, v, c = lax.axis_index("root"), lax.axis_index("virt"), lax.axis_index("occ")
     mate = 1 - c
     groups, parts, per, batch = s.groups, s.parts, s.per, s.batch
     home, place = z // per, z % per
     at_home = home == c
+    beside = home * per + 1 - place
+    opposite = lax.rem(z + per, groups)
+
+    slot_of, count = [], jnp.int32(0)
+    for n in range(s.roots):
+        live = 1 - converged[n]
+        slot_of.append(jnp.where(live == 1, count, -1))
+        count = count + live
+
+    def slots_at(group):
+        found = []
+        for r in range(s.local):
+            value = slot_of[r]
+            for g in range(1, groups):
+                value = jnp.where(group == g, slot_of[g * s.local + r], value)
+            found.append(value)
+        return found
+
+    my_slots, near_slots = slots_at(z), slots_at(beside)
+    weights = [jnp.where(value >= 0, 1.0, 0.0) for value in my_slots]
+
+    def choose(number, values):
+        result = values[0]
+        for k in range(1, len(values)):
+            result = lax.select(number == k, values[k], result)
+        return result
+
+    def of_half(k, inside, beyond):
+        value = beyond
+        for r in range(s.local):
+            value = lax.select(my_slots[r] == k, inside[r], value)
+            value = lax.select(near_slots[r] == k, inside[s.local + r], value)
+        return value
 
     def turn(index, by, size):
         return lax.rem(index + by, size)
@@ -217,38 +253,42 @@
     def slab_rows(u):
         return pl.ds(u * s.tiles, s.tiles)
 
-    def slab_copy(d, r):
+    def share(u, i):
+        start = (u // CORES) * s.piece + i * s.tile + lax.rem(u, CORES) * s.slab
+        return pl.ds(pl.multiple_of(start, 128), s.slab)
+
+    def slab_copy(i, d, r):
         u = turn(v, d, parts)
         return remote(
-            trial.at[r, :, :, lanes(u, s.slab)], slab.at[r, slab_rows(v)],
-            s_vin.at[d, r], r_vin.at[v, r], virt=u,
-        )
-
-    def slab_own(r):
+            trial.at[r, :, :, share(u, i)], slab.at[i, r, slab_rows(v)],
+            s_vin.at[i, d, r], r_vin.at[i, v, r], virt=u,
+        )
+
+    def slab_own(i, r):
         return pltpu.make_async_copy(
-            trial.at[r, :, :, lanes(v, s.slab)], slab.at[r, slab_rows(v)], r_vin.at[v, r]
-        )
-
-    def slab_got(d, r):
+            trial.at[r, :, :, share(v, i)], slab.at[i, r, slab_rows(v)], r_vin.at[i, v, r]
+        )
+
+    def slab_got(i, d, r):
+        u = turn(v, d, parts)
+        spot = slab.at[i, r, slab_rows(u)]
+        return remote(spot, spot, s_vin.at[i, d, r], r_vin.at[i, u, r], virt=u)
+
+    def back_copy(i, d):
+        return remote(
+            product.at[i, d - 1], vv.at[v, i],
+            s_vout.at[i, d], r_vout.at[i, v], virt=turn(v, d, parts),
+        )
+
+    def back_got(i, d):
         u = turn(v, d, parts)
         return remote(
-            slab.at[r, slab_rows(u)], slab.at[r, slab_rows(u)],
-            s_vin.at[d, r], r_vin.at[u, r], virt=u,
-        )
-
-    def back_copy(d, r):
-        u = turn(v, d, parts)
-        return remote(
-            product.at[d, r], vv.at[r, :, :, lanes(v, s.slab)],
-            s_vout.at[d, r], r_vout.at[v, r], virt=u,
-        )
-
-    def back_got(d, r):
-        u = turn(v, d, parts)
-        return remote(
-            product.at[d, r], vv.at[r, :, :, lanes(u, s.slab)],
-            s_vout.at[d, r], r_vout.at[u, r], virt=u,
-        )
+            product.at[i, d - 1], vv.at[u, i], s_vout.at[i, d], r_vout.at[i, u], virt=u
+        )
+
+    def vv_at(r, tile, j, i):
+        parts_of = [vv[j * CORES + h, i, r, tile] for h in range(CORES)]
+        return jnp.concatenate([p.astype(jnp.float32) for p in parts_of], axis=1)
 
     def load(source, t, slot):
         return pltpu.make_async_copy(
@@ -260,37 +300,28 @@
             sent.at[:, cut(t)], got.at[:, cut(t)], s_cor.at[t], r_cor.at[t], occ=mate
         )
 
-    def outer_copy(t, d):
-        to = turn(z, d, groups)
+    def third(i, quarter=0):
+        return lanes(quarter * s.thirds + i, s.tile)
+
+    def near_copy(i):
         return remote(
-            summed.at[to, cut(t)], outer.at[c, cut(t), :, lanes(place, s.piece)],
-            s_out.at[t, d], r_out.at[t, place, c], root=to, occ=home,
-        )
-
-    def outer_got(t, j, r):
-        src = c * per + j
-        core = jnp.where(src == z, mate, r)
-        spot = outer.at[r, cut(t), :, lanes(j, s.piece)]
-        return remote(spot, spot, s_out.at[t, 0], r_out.at[t, j, r], root=src, occ=core)
-
-    def sigma_copy(t, r, j):
-        to = c * per + j
-        return remote(
-            sigma.at[r, cut(t), :, lanes(j, s.piece)], sigmas.at[z, cut(t)],
-            s_sig.at[t, r, j], r_sig.at[t, z], root=to, occ=r,
-        )
-
-    def sigma_got(t, d):
-        src = turn(z, d, groups)
-        core = jnp.where(src == z, mate, home)
-        return remote(
-            sigmas.at[src, cut(t)], sigmas.at[src, cut(t)],
-            s_sig.at[t, 0, 0], r_sig.at[t, src], root=src, occ=core,
-        )
-
-    def result_copy(t, r):
+            rest.at[(1 - place) * s.thirds + i], near.at[i],
+            s_near.at[i], r_near.at[i], root=beside,
+        )
+
+    def far_copy(i):
+        return remote(across.at[i], far.at[i], s_far.at[i], r_far.at[i], root=opposite)
+
+    def pass_copy(i):
+        return remote(far.at[i], far.at[i], s_pass.at[i], r_pass.at[i], occ=mate)
+
+    def hand_copy(i):
+        return remote(handed.at[i], taken.at[i], s_hand.at[i], r_hand.at[i], root=beside)
+
+    def result_copy(i, r, j):
+        here = third(i, j)
         return pltpu.make_async_copy(
-            sigma.at[r, cut(t)], sigma_out.at[r, cut(t)], s_res.at[t, r]
+            sigma.at[r, :, :, here], sigma_out.at[r, :, :, here], s_res.at[i, r, j]
         )
 
     barrier = pltpu.get_barrier_semaphore()
@@ -330,10 +361,14 @@
         for r in range(s.local):
             trial_own(r).start()
 
-    for r in range(s.local):
-        for d in range(1, parts):
-            slab_copy(d, r).start()
-        slab_own(r).start()
+    def slab_start(i):
+        for r in range(s.local):
+            for d in range(1, parts):
+                slab_copy(i, d, r).start()
+            slab_own(i, r).start()
+
+    for i in range(s.thirds - 1):
+        slab_start(i)
     swap_copy().start()
     own_copy = pltpu.make_async_copy(flat_trial, own, s_own)
     own_copy.start()
@@ -365,14 +400,14 @@
     everyones = sall[0]
     for g in range(1, groups):
         everyones = everyones + sall[g]
-    left = iota((s.roots * ROWS, s.roots), 0) // ROWS
-    chosen = jnp.where(
-        left < groups, s.local * left + c, s.local * (left - groups) + mate
-    )
-    left = one_hot(iota((s.roots * ROWS, s.roots), 1) == chosen, jnp.bfloat16)
+    shape = (s.slots * ROWS, s.roots)
+    left = iota(shape, 0) < 0
+    for n in range(s.roots):
+        left = left | ((iota(shape, 0) // ROWS == slot_of[n]) & (iota(shape, 1) == n))
+    left = one_hot(left, jnp.bfloat16)
     right = iota((128, s.half * ROWS), 1) // ROWS + c * s.half
     right = one_hot(iota((128, s.half * ROWS), 0) == right, jnp.bfloat16)
-    shape = (s.roots * ROWS, s.half * ROWS)
+    shape = (s.slots * ROWS, s.half * ROWS)
     mixed = dot(dot(left, everyones.astype(jnp.bfloat16)).astype(jnp.bfloat16), right)
     same = iota(shape, 0) % ROWS == iota(shape, 1) % ROWS
     mix[...] = jnp.where(same, -mixed, 0.0).astype(jnp.bfloat16)
@@ -385,18 +420,20 @@
             summed[:, tile] = (kept[slot, :, g] + got[:, tile].astype(jnp.float32)).astype(
                 jnp.bfloat16
             )
-        for d in range(1, groups):
-            outer_copy(t, d).start()
-
-        @pl.when(at_home)
-        def _():
-            for g in range(batch):
-                tile = t * batch + g
-                outer[c, tile, :, lanes(place, s.piece)] = summed[z, tile]
-
-        @pl.when(jnp.logical_not(at_home))
-        def _():
-            outer_copy(t, 0).start()
+
+    def virtual(i):
+        for r in range(s.local):
+            for d in range(1, parts):
+                slab_got(i, d, r).wait_recv()
+            slab_own(i, r).wait()
+            amps = flat(slab[i, r])
+            for d in range(1, parts):
+                part = dot(virt_fock[turn(v, d, parts)], amps)
+                product[i, d - 1, r] = part.reshape(s.tiles, ROWS, s.slab).astype(jnp.bfloat16)
+            part = dot(virt_fock[v], amps).reshape(s.tiles, ROWS, s.slab)
+            vv[v, i, r] = part.astype(jnp.bfloat16)
+        for d in range(1, parts):
+            back_copy(i, d).start()
 
     def outer_step(t, carry):
         slot = lax.rem(t, 2)
@@ -408,20 +445,26 @@
         load(ovoo, t, slot).wait()
         for g in range(batch):
             value = dot(mix[...], flat(blocks[slot, :, g]))
-            value = value.reshape(s.roots, ROWS, s.piece)
-            kept[slot, :, g] = value[:groups]
-            sent[:, t * batch + g] = value[groups:].astype(jnp.bfloat16)
+            value = value.reshape(s.slots, ROWS, s.piece)
+            kept[slot, :, g] = value
+            sent[:, t * batch + g] = value.astype(jnp.bfloat16)
         core_copy(t).start()
 
         @pl.when(t > 0)
         def _():
             finish(t - 1)
+
+        @pl.when(t == s.steps // 2)
+        def _():
+            virtual(0)
+            slab_start(s.thirds - 1)
 
         return carry
 
     lax.fori_loop(0, s.steps, outer_step, 0)
     finish(s.steps - 1)
     load(ooov, 0, 0).start()
+    lax.fori_loop(1, s.thirds - 1, lambda i, carry: (virtual(i), carry)[1], 0)
 
     own_copy.wait()
     swap_copy().wait_recv()
@@ -448,99 +491,165 @@
 
         return lax.fori_loop(0, columns, inner, carry)
 
-    early = columns // 3
-    lax.fori_loop(0, early, column, 0)
-    for r in range(s.local):
+    def each_tile(body):
+        def step(tile, carry):
+            body(tile)
+            return carry
+
+        lax.fori_loop(0, s.tiles, step, 0)
+
+    def rows_of(r, tile):
+        return pl.ds(pl.multiple_of(r * s.rows + tile * ROWS, ROWS), ROWS)
+
+    def summed_at(k, tile, i):
+        return summed[k, tile, :, third(i)]
+
+    def far_at(k, tile, i):
+        return far[i, k, tile]
+
+    def hand(source, i):
+        def body(tile):
+            values = [source(k, tile, i) for k in range(s.slots)]
+            for r in range(s.local):
+                handed[i, r, tile] = choose(near_slots[r], values)
+
+        each_tile(body)
+        hand_copy(i).start()
+
+    def inside_at(tile, i):
+        own_part = [rest[place * s.thirds + i, r, tile] for r in range(s.local)]
+        return own_part + [near[i, r, tile] for r in range(s.local)]
+
+    def cross(i):
+        near_copy(i).wait_recv()
+
+        @pl.when(at_home)
+        def _():
+            hand(summed_at, i)
+
+        @pl.when(jnp.logical_not(at_home))
+        def _():
+            def body(tile):
+                inside = inside_at(tile, i)
+                for k in range(s.slots):
+                    across[i, k, tile] = of_half(k, inside, summed_at(k, tile, i))
+
+            each_tile(body)
+            far_copy(i).start()
+
+    def rest_step(i, carry):
+        def quarter(j, carry):
+            @pl.when((j == 1) & (i > 0))
+            def _():
+                cross(i - 1)
+
+            @pl.when((j == 1) & (i == 0))
+            def _():
+                virtual(s.thirds - 1)
+
+            return column(j * s.thirds + i, carry)
+
+        lax.fori_loop(0, per, quarter, 0)
         for d in range(1, parts):
-            slab_got(d, r).wait_recv()
-        slab_own(r).wait()
-    for r in range(s.local):
-        amps = flat(slab[r])
-        for d in range(1, parts):
-            part = dot(virt_fock[turn(v, d, parts)], amps)
-            product[d, r] = part.reshape(s.tiles, ROWS, s.slab).astype(jnp.bfloat16)
-            back_copy(d, r).start()
-        part = dot(virt_fock[v], amps).reshape(s.tiles, ROWS, s.slab)
-        vv[r, :, :, lanes(v, s.slab)] = part.astype(jnp.bfloat16)
-    lax.fori_loop(early, columns, column, 0)
-
+            back_got(i, d).wait_recv()
+
+        def body(tile):
+            for r in range(s.local):
+                for j in range(per):
+                    value = vv_at(r, tile, j, i) - oo[rows_of(r, tile), third(i, j)]
+                    rest[j * s.thirds + i, r, tile] = value.astype(jnp.bfloat16)
+
+        each_tile(body)
+        near_copy(i).start()
+        return carry
+
+    lax.fori_loop(0, s.thirds, rest_step, 0)
+    cross(s.thirds - 1)
+
+    table[...] = jnp.zeros_like(table)
+    square[...] = jnp.zeros_like(square)
+
+    def coupling_step(t, carry):
+        slot = lax.rem(t, 2)
+
+        @pl.when(t + 1 < s.steps)
+        def _():
+            load(ooov, t + 1, 1 - slot).start()
+
+        load(ooov, t, slot).wait()
+        for g in range(batch):
+            table[...] += dot_t(flat(everyone[:, t * batch + g]), flat(blocks[slot, :, g]))
+        return carry
+
+    def forward(i):
+        @pl.when(at_home)
+        def _():
+            far_copy(i).wait_recv()
+            pass_copy(i).start()
+
+        @pl.when(jnp.logical_not(at_home))
+        def _():
+            pass_copy(i).wait_recv()
+            hand(far_at, i)
+
+    def sigma_step(i):
+        hand_copy(i).wait_recv()
+
+        def finish_tile(source):
+            def body(tile):
+                values = [source(k, tile, i) for k in range(s.slots)]
+                for r in range(s.local):
+                    mine = choose(my_slots[r], values)
+                    for j, outer in ((place, mine), (1 - place, taken[i, r, tile])):
+                        here = third(i, j)
+                        value = (
+                            vv_at(r, tile, j, i)
+                            + outer.astype(jnp.float32)
+                            - oo[rows_of(r, tile), here]
+                        )
+                        sigma[r, tile, :, here] = (weights[r] * value).astype(jnp.bfloat16)
+
+            each_tile(body)
+
+        @pl.when(at_home)
+        def _():
+            finish_tile(summed_at)
+
+        @pl.when(jnp.logical_not(at_home))
+        def _():
+            finish_tile(far_at)
+
+        for r in range(s.local):
+            for j in range(per):
+                result_copy(i, r, j).start()
+
+    for i in range(s.thirds - 1):
+        forward(i)
     for d in range(1, groups):
         trial_got(turn(z, d, groups) * s.local + c).wait_recv()
         trial_pass(d).start()
-    for r in range(s.local):
-        for d in range(1, parts):
-            back_got(d, r).wait_recv()
-
-    def sigma_step(t, carry):
-        for r in range(s.local):
-            for j in range(per):
-                @pl.when(jnp.logical_not((c * per + j == z) & (c == r)))
-                def _():
-                    outer_got(t, j, r).wait_recv()
-
-            for g in range(batch):
-                tile = t * batch + g
-                rows = pl.ds(pl.multiple_of(r * s.rows + tile * ROWS, ROWS), ROWS)
-                value = (
-                    vv[r, tile].astype(jnp.float32)
-                    + outer[r, tile].astype(jnp.float32)
-                    - oo[rows, :]
-                )
-                sigma[r, tile] = (active[z * s.local + r] * value).astype(jnp.bfloat16)
-            result_copy(t, r).start()
-            for j in range(per):
-                here = (c * per + j == z) & (c == r)
-
-                @pl.when(jnp.logical_not(here))
-                def _():
-                    sigma_copy(t, r, j).start()
-
-                @pl.when(here)
-                def _():
-                    for g in range(batch):
-                        tile = t * batch + g
-                        sigmas[z, tile] = sigma[r, tile, :, j * s.piece : (j + 1) * s.piece]
-
-        return carry
-
-    lax.fori_loop(0, s.steps, sigma_step, 0)
-
     for d in range(1, groups):
         trial_got(turn(z, d, groups) * s.local + mate).wait_recv()
     for r in range(s.local):
         trial_got(z * s.local + r).wait_recv()
-    table[...] = jnp.zeros_like(table)
-    square[...] = jnp.zeros_like(square)
-
-    def coupling_step(t, carry):
-        slot = lax.rem(t, 2)
-
-        @pl.when(t + 1 < s.steps)
-        def _():
-            load(ooov, t + 1, 1 - slot).start()
-
-        load(ooov, t, slot).wait()
-        for g in range(batch):
-            table[...] += dot_t(flat(everyone[:, t * batch + g]), flat(blocks[slot, :, g]))
-        return carry
 
     lax.fori_loop(0, s.steps, coupling_step, 0)
-
-    def project_step(t, carry):
-        for d in range(groups):
-            if d:
-                sigma_got(t, d).wait_recv()
-            else:
-                @pl.when(jnp.logical_not(at_home))
-                def _():
-                    sigma_got(t, 0).wait_recv()
-
-        for g in range(batch):
-            tile = t * batch + g
-            square[...] += dot_t(flat(everyone[:, tile]), flat(sigmas[:, tile]))
-        return carry
-
-    lax.fori_loop(0, s.steps, project_step, 0)
+    forward(s.thirds - 1)
+
+    @pl.when(at_home)
+    def _():
+        def body(tile):
+            for i in range(s.thirds):
+                inside = inside_at(tile, i)
+                values = [
+                    summed_at(k, tile, i).astype(jnp.float32)
+                    + of_half(k, inside, far_at(k, tile, i)).astype(jnp.float32)
+                    for k in range(s.slots)
+                ]
+                values = jnp.concatenate(values, axis=0).astype(jnp.bfloat16)
+                square[...] += dot_t(flat(everyone[:, tile, :, third(i)]), values)
+
+        each_tile(body)
 
     gather = one_hot(iota((s.roots, s.roots * ROWS), 1) // ROWS == iota((s.roots, s.roots * ROWS), 0))
 
@@ -548,11 +657,17 @@
         rows = iota(values.shape, 0) % ROWS == iota(values.shape, 1) % ROWS
         folded = dot(gather, jnp.where(rows, values, 0.0), HIGH)
         width = values.shape[1]
-        to = target(iota((width, 128), 0) // ROWS)
-        return dot(folded, one_hot(iota((width, 128), 1) == to), HIGH)
-
-    part = same_row(table[...], lambda k: c * s.half + k)
-    part = part + same_row(square[...], lambda o: s.occ + s.local * o + c)
+        to = target(iota((width, 128), 0) // ROWS, iota((width, 128), 1))
+        return dot(folded, one_hot(to), HIGH)
+
+    def root_lane(k, lane):
+        found = lane < 0
+        for n in range(s.roots):
+            found = found | ((k == slot_of[n]) & (lane == s.occ + n))
+        return found
+
+    part = same_row(table[...], lambda k, lane: lane == c * s.half + k)
+    part = part + same_row(square[...], root_lane)
 
     def summed_over(held, index, size, base, name):
         def copy(d):
@@ -570,25 +685,34 @@
 
         for d in range(1, size):
             copy(d).start()
-        for d in range(1, size):
-            got_from(d).wait_recv()
-        total = held[0]
-        for g in range(1, size):
-            total = total + held[g]
+
+        def total():
+            for d in range(1, size):
+                got_from(d).wait_recv()
+            value = held[0]
+            for g in range(1, size):
+                value = value + held[g]
+            return value
+
         return total, copy
 
     red0[c] = part
     total, copy0 = summed_over(red0, c, CORES, 0, "occ")
-    red1[v] = total
+    for i in range(s.thirds - 1):
+        sigma_step(i)
+    red1[v] = total()
     total, copy1 = summed_over(red1, v, parts, CORES, "virt")
-    red2[z] = total
+    sigma_step(s.thirds - 1)
+    red2[z] = total()
     total, copy2 = summed_over(red2, z, groups, CORES + parts, "root")
+    total = total()
 
     coupling = total[:, : s.occ]
     ones = everyones[:, : s.occ]
     weight = jnp.zeros((s.roots, 1), jnp.float32)
     for n in range(s.roots):
-        weight = jnp.where(iota((s.roots, 1), 0) == n, active[n], weight)
+        live = jnp.where(slot_of[n] >= 0, 1.0, 0.0)
+        weight = jnp.where(iota((s.roots, 1), 0) == n, live, weight)
     every = weight * (-dot(ones.astype(jnp.bfloat16), occ_fock[...]) - 0.5 * coupling)
     whole = total[:, s.occ : s.occ + s.roots] / math.sqrt(s.occ * s.occ * s.virt)
     whole = whole + dot_t(ones, every, HIGH) / math.sqrt(s.occ)
@@ -604,41 +728,46 @@
         copy2(d).wait_send()
     for d in range(1, parts):
         copy1(d).wait_send()
-        for r in range(s.local):
-            slab_copy(d, r).wait_send()
-            back_copy(d, r).wait_send()
     copy0(1).wait_send()
     swap_copy().wait_send()
     for j in range(per):
         for r in range(s.local):
             trial_copy(j, r).wait_send()
 
-    def drain(t, carry):
+    def drain_core(t, carry):
         core_copy(t).wait_send()
-        for d in range(1, groups):
-            outer_copy(t, d).wait_send()
+        return carry
+
+    lax.fori_loop(0, s.steps, drain_core, 0)
+
+    def drain(i, carry):
+        for r in range(s.local):
+            for d in range(1, parts):
+                slab_copy(i, d, r).wait_send()
+            for j in range(per):
+                result_copy(i, r, j).wait()
+        for d in range(1, parts):
+            back_copy(i, d).wait_send()
+        near_copy(i).wait_send()
+        hand_copy(i).wait_send()
+
+        @pl.when(at_home)
+        def _():
+            pass_copy(i).wait_send()
 
         @pl.when(jnp.logical_not(at_home))
         def _():
-            outer_copy(t, 0).wait_send()
-
-        for r in range(s.local):
-            result_copy(t, r).wait()
-            for j in range(per):
-                @pl.when(jnp.logical_not((c * per + j == z) & (c == r)))
-                def _():
-                    sigma_copy(t, r, j).wait_send()
+            far_copy(i).wait_send()
 
         return carry
 
-    lax.fori_loop(0, s.steps, drain, 0)
+    lax.fori_loop(0, s.thirds, drain, 0)
 
 
 def local(trial_singles, trial_doubles, occ_fock, virt_fock, w_ovoo, w_ooov, converged):
     if not fits(trial_doubles, occ_fock, virt_fock, converged):
         return plain(trial_singles, trial_doubles, occ_fock, virt_fock, w_ovoo, w_ooov, converged)
     s = Sizes(trial_doubles, occ_fock, virt_fock, converged)
-    active = (1 - converged).astype(jnp.float32)
     trial = trial_doubles.reshape(s.local, s.tiles, ROWS, s.pairs)
     flat_trial = trial_doubles.reshape(s.local * s.rows, s.pairs)
     fock = virt_fock.reshape(s.parts, s.rows, s.virt)
@@ -649,7 +778,7 @@
     vmem = pl.BlockSpec(memory_space=pltpu.VMEM)
     smem = pl.BlockSpec(memory_space=pltpu.SMEM)
     dma, n = pltpu.SemaphoreType.DMA, s.roots * ROWS
-    wide_tile = (s.tiles, ROWS, s.piece)
+    wide_tile, third_tile = (s.tiles, ROWS, s.piece), (s.tiles, ROWS, s.tile)
     sigma, singles, matrix = pl.pallas_call(
         functools.partial(whole_body, s),
         in_specs=[smem, vmem, anywhere, anywhere, vmem, vmem, anywhere, anywhere],
@@ -661,40 +790,46 @@
         ],
         scratch_shapes=[
             pltpu.VMEM((s.groups, ROWS, 128), f32),
-            pltpu.VMEM((n, s.half * ROWS), bf),
+            pltpu.VMEM((s.slots * ROWS, s.half * ROWS), bf),
             pltpu.VMEM((s.occ, s.tile), f32),
             pltpu.VMEM((s.tile, s.tile), bf),
             pltpu.VMEM((s.occ, s.pairs), f32),
             pltpu.VMEM((s.tile, s.tile), bf),
             pltpu.VMEM(flat_trial.shape, bf),
             pltpu.VMEM(flat_trial.shape, bf),
-            pltpu.VMEM((s.local, s.parts * s.tiles, ROWS, s.slab), bf),
-            pltpu.VMEM((s.parts, s.local, s.tiles, ROWS, s.slab), bf),
-            pltpu.VMEM(trial.shape, bf),
+            pltpu.VMEM((s.thirds, s.local, s.parts * s.tiles, ROWS, s.slab), bf),
+            pltpu.VMEM((s.thirds, s.parts - 1, s.local, s.tiles, ROWS, s.slab), bf),
+            pltpu.VMEM((s.parts, s.thirds, s.local, s.tiles, ROWS, s.slab), bf),
             pltpu.VMEM((s.roots,) + wide_tile, bf),
             pltpu.VMEM((2, s.half, s.batch, ROWS, s.piece), bf),
-            pltpu.VMEM((2, s.groups, s.batch, ROWS, s.piece), f32),
-            pltpu.VMEM((s.groups,) + wide_tile, bf),
-            pltpu.VMEM((s.groups,) + wide_tile, bf),
-            pltpu.VMEM((s.groups,) + wide_tile, bf),
-            pltpu.VMEM(trial.shape, bf),
+            pltpu.VMEM((2, s.slots, s.batch, ROWS, s.piece), f32),
+            pltpu.VMEM((s.slots,) + wide_tile, bf),
+            pltpu.VMEM((s.slots,) + wide_tile, bf),
+            pltpu.VMEM((s.slots,) + wide_tile, bf),
             pltpu.VMEM(flat_trial.shape, f32),
             pltpu.VMEM(trial.shape, bf),
-            pltpu.VMEM((s.groups,) + wide_tile, bf),
+            pltpu.VMEM((s.per * s.thirds, s.local) + third_tile, bf),
+            pltpu.VMEM((s.thirds, s.local) + third_tile, bf),
+            pltpu.VMEM((s.thirds, s.slots) + third_tile, bf),
+            pltpu.VMEM((s.thirds, s.slots) + third_tile, bf),
+            pltpu.VMEM((s.thirds, s.local) + third_tile, bf),
+            pltpu.VMEM((s.thirds, s.local) + third_tile, bf),
             pltpu.VMEM((n, s.half * ROWS), f32),
-            pltpu.VMEM((n, s.groups * ROWS), f32),
+            pltpu.VMEM((n, s.slots * ROWS), f32),
             pltpu.VMEM((CORES, ROWS, 128), f32),
             pltpu.VMEM((s.parts, ROWS, 128), f32),
             pltpu.VMEM((s.groups, ROWS, 128), f32),
             dma((s.groups,)), dma((s.groups,)),
             dma((s.per, s.local)), dma((s.roots,)), dma((s.groups,)), dma(()),
             dma(()), dma(()),
-            dma((s.parts, s.local)), dma((s.parts, s.local)),
-            dma((s.parts, s.local)), dma((s.parts, s.local)),
+            dma((s.thirds, s.parts, s.local)), dma((s.thirds, s.parts, s.local)),
+            dma((s.thirds, s.parts)), dma((s.thirds, s.parts)),
             dma((2,)), dma((s.steps,)), dma((s.steps,)),
-            dma((s.steps, s.groups)), dma((s.steps, s.per, s.local)),
-            dma((s.steps, s.local, s.per)), dma((s.steps, s.groups)),
-            dma((s.steps, s.local)),
+            dma((s.thirds,)), dma((s.thirds,)),
+            dma((s.thirds,)), dma((s.thirds,)),
+            dma((s.thirds,)), dma((s.thirds,)),
+            dma((s.thirds,)), dma((s.thirds,)),
+            dma((s.thirds, s.local, s.per)),
             dma((CORES + s.parts + s.groups,)), dma((CORES + s.parts + s.groups,)),
         ],
         compiler_params=pltpu.CompilerParams(
@@ -704,7 +839,7 @@
             flops=8 * s.rows * s.pairs * s.pairs, bytes_accessed=4 * w_ovoo.size, transcendentals=0
         ),
         name="sigma_step",
-    )(active, trial_singles, trial, flat_trial, occ_fock, fock, outer_in, coupling_in)
+    )(converged, trial_singles, trial, flat_trial, occ_fock, fock, outer_in, coupling_in)
     return (sigma.reshape(trial_doubles.shape), singles, matrix)
 
 

time: 169 us -> 152 us (0.90)
  Pallas kernels: 163 us -> 146 us
    pallas_call x1, Pallas kernels: 163 us -> 146 us  [local(): pl.pallas_call(functools.partial(whole_body, s), in_specs=[smem, vmem, an...]
where the time goes in v2:
time: 152 us; the launch traced here: 151 us
  Pallas kernels  146 us (96%)
  local copies, waits for them, and re-layouts  4.26 us (3%)
    pallas_call x1, Pallas kernels, local(): pl.pallas_call(functools.partial(whole_body, s), in_specs=[smem, vmem, an...  146 us
    unnamed x7, local copies, waits for them, and re-layouts  4.26 us

profile of v2, /device:TPU:0, one launch (start us, length us, event | category | flops | bytes accessed | tf_op | source)
XLA Modules:
  0.0 150.8 jit_solution(11285220978184042585)
XLA Ops:
  0.6 145.9 %sigma_step.1 = (bf16[2,15,8,4608]{3,2,1,0:T(8,128)(2,1)}, f32[2,96]{1,0:T(2,128)}, f32[2,8]{1,0:T(2,128)}) custom-call(s32[8]{0:T(128)} %converged.1, bf16[2,96]{1,0:T(2,128)(2,1)} %singles.1, bf16[2,15,8,4608]{3,2,1,0:T(8,128)(2,1)} %bitcast.9, bf16[240,4608]{1,0:T(8,128)(2,1)} %bitcast.10, bf16[96,96]{1,0:T(8,128)(2,1)} %occ_fock.1, ...), custom_call_target="tpu_custom_call" | custom-call | flops 20384317440 | bytes 53084160 | tf_op jit(solution)/shard_map/sigma_step/pallas_call | solution.py:782
  146.6 0.0 copy-start.1
  146.6 0.0 copy-start
  146.6 3.1 %copy.13 = bf16[2,120,4608]{2,1,0:T(8,128)(2,1)} copy(bf16[2,120,4608]{2,1,0:T(8,128)(2,1)} %bitcast.6) | data formatting | bytes 4423680
  149.7 0.0 copy-done.1
  149.7 0.6 copy.14
  150.3 0.0 copy-done
  150.3 0.6 copy.15
Async XLA Ops:
  146.6 3.1 %copy-start.1 = (f32[2,96]{1,0:T(2,128)S(1)}, f32[2,96]{1,0:T(2,128)}, u32[]{:S(2)}) copy-start(f32[2,96]{1,0:T(2,128)} %get-tuple-element.13) | copy-start | bytes 2308
  146.6 3.7 %copy-start = (f32[2,8]{1,0:T(2,128)S(1)}, f32[2,8]{1,0:T(2,128)}, u32[]{:S(2)}) copy-start(f32[2,8]{1,0:T(2,128)} %get-tuple-element.14) | copy-start | bytes 196
